TPU v7x, 32 devices: a whole 2x2x4 slice. The times are simulated.
32 devices in a mesh: dp: 2 (over x), expert: 16 (over z, y, core).
Axes of the slice: x: 2, y: 2, z: 4, core: 2. Of those that a mesh axis runs over, the one named last changes fastest.
Arguments:
- tokens: bfloat16 [4096, 512], P(('dp', 'expert')), may hold values from -6 to 6
- cotangent: bfloat16 [4096, 512], P(('dp', 'expert')), may hold values from -0.29882812 to 0.29882812
- labels: int32 [4096, 1], P(('dp', 'expert')), may hold values from 0 to 31; in each aligned block of 128 rows (0 to 127, 128 to 255, ...) at most 4 rows name the same one
- placement: int32 [32], replicated, may hold values from 0 to 31, each once
- mass: float32 [4096], P(('dp', 'expert')), may hold values from 0.1 to 10
- w_head: float32 [512, 16], replicated, may hold values from -0.25 to 0.25
- w_up: bfloat16 [32, 512, 2048], P('expert', None, 'dp'), may hold values from -0.25 to 0.25
- w_down: bfloat16 [32, 2048, 512], P('expert', 'dp'), may hold values from -0.125 to 0.125
- up_moment: bfloat16 [32, 512, 2048], P('expert', None, 'dp'), may hold values from -2 to 2
- up_square: bfloat16 [32, 512, 2048], P('expert', None, 'dp'), may hold values from 0.0099487305 to 1
- down_moment: bfloat16 [32, 2048, 512], P('expert', 'dp'), may hold values from -2 to 2
- down_square: bfloat16 [32, 2048, 512], P('expert', 'dp'), may hold values from 0.0099487305 to 1
Outputs:
- fine_precip: float32 [4096, 16], P(('dp', 'expert'))
- up_next: bfloat16 [32, 512, 2048], P('expert', None, 'dp')
- down_next: bfloat16 [32, 2048, 512], P('expert', 'dp')
- up_moment_next: bfloat16 [32, 512, 2048], P('expert', None, 'dp')
- up_square_next: bfloat16 [32, 512, 2048], P('expert', None, 'dp')
- down_moment_next: bfloat16 [32, 2048, 512], P('expert', 'dp')
- down_square_next: bfloat16 [32, 2048, 512], P('expert', 'dp')
Inputs may be any that keep to these rules, and one draw needn't show every extreme that they name: `labels`: within each device's block of 128 rows no regime is named more than 4 times, and in every draw some regime is named exactly 4 times in some block; every regime is named somewhere. `placement`: each regime stands in exactly one expert slot.
All inputs are finite; a program needn't handle non-finite values.
Results may differ from a plain program's by a relative error of at most 0.0045.
Values may be sent and summed in bfloat16 or wider, within the bound.
No kernel may reach another device: no remote copies, remote signals or barrier semaphores. Data moves between devices by JAX's collectives and lax.ppermute only.
A program may use at most 64 MiB of HBM per device.

v0:
```python
import jax
import jax.numpy as jnp
from jax import lax
from jax.sharding import PartitionSpec as P

CAP = 4


beta_first = 0.9
beta_second = 0.95
correct_first = 1.0 - 0.9**20
correct_second = 1.0 - 0.95**20
learn_rate = 0.002
adam_epsilon = 1e-08


def gelu_parts(pre):
    normal_cdf = 0.5 * (1.0 + lax.erf(pre * 0.7071067811865476))
    density = jnp.exp(-0.5 * pre * pre) * 0.3989422804014327
    return (pre * normal_cdf, normal_cdf + pre * density)


def adam_step(weight, first, second, grad):
    new_first = beta_first * first.astype(jnp.float32) + (1.0 - beta_first) * grad
    new_second = beta_second * second.astype(jnp.float32) + (1.0 - beta_second) * grad * grad
    update = new_first / correct_first / (jnp.sqrt(new_second / correct_second) + adam_epsilon)
    moved = weight.astype(jnp.float32) - learn_rate * update
    return (
        moved.astype(jnp.bfloat16),
        new_first.astype(jnp.bfloat16),
        new_second.astype(jnp.bfloat16),
    )


def route_slots(labels, placement, capacity, holders, local_count):
    experts = placement.shape[0]
    regimes = jnp.arange(experts, dtype=jnp.int32)
    owner = jnp.sum(jnp.where(placement[None, :] == regimes[:, None], regimes[None, :], 0), axis=1)
    chosen = labels[:, 0][:, None] == regimes[None, :]
    target = jnp.sum(jnp.where(chosen, owner[None, :], 0), axis=1)
    onehot = (target[:, None] == regimes[None, :]).astype(jnp.int32)
    earlier = jnp.cumsum(onehot, axis=0) - onehot
    position = jnp.sum(earlier * onehot, axis=1)
    lane_index = target % local_count * holders + target // local_count
    return lane_index * capacity + position


def fill_slots(values, slots, count):
    row_count = values.shape[0]
    source = (
        jnp.full((count,), row_count, jnp.int32)
        .at[slots]
        .set(jnp.arange(row_count, dtype=jnp.int32))
    )
    padded = jnp.concatenate([values, jnp.zeros((1, values.shape[1]), values.dtype)], axis=0)
    return jnp.take(padded, source, axis=0)


def expert_rows(rows_x, rows_grad, w_in, w_out):
    pre = jnp.einsum("krd,kdf->krf", rows_x, w_in, preferred_element_type=jnp.float32)
    value, slope = gelu_parts(pre)
    hidden = value.astype(jnp.bfloat16)
    back = jnp.einsum("krd,kfd->krf", rows_grad, w_out, preferred_element_type=jnp.float32)
    hidden_grad = (back * slope).astype(jnp.bfloat16)
    return (hidden, hidden_grad)


def outer_in(rows_x, hidden_grad):
    return jnp.einsum("krd,krf->kdf", rows_x, hidden_grad, preferred_element_type=jnp.float32)


def outer_out(hidden, rows_grad):
    return jnp.einsum("krf,krd->kfd", hidden, rows_grad, preferred_element_type=jnp.float32)


def local(
    tokens,
    cotangent,
    labels,
    placement,
    mass,
    w_head,
    w_up,
    w_down,
    up_moment,
    up_square,
    down_moment,
    down_square,
):
    capacity = CAP
    experts = placement.shape[0]
    width = tokens.shape[1]
    local_count = w_up.shape[0]
    holders = lax.axis_size("expert")
    slots = route_slots(labels, placement, capacity, holders, local_count)
    slot_count = experts * capacity
    recv_rows = holders * capacity
    send_x = fill_slots(tokens, slots, slot_count).reshape(local_count, holders, capacity, width)
    send_grad = fill_slots(cotangent, slots, slot_count).reshape(
        local_count, holders, capacity, width
    )
    recv_x, recv_grad = (
        lax.all_to_all(send_x, "expert", split_axis=1, concat_axis=1, tiled=True),
        lax.all_to_all(send_grad, "expert", split_axis=1, concat_axis=1, tiled=True),
    )
    recv_x = recv_x.reshape(local_count, recv_rows, width)
    recv_grad = recv_grad.reshape(local_count, recv_rows, width)
    piece_x = lax.all_gather(recv_x, "dp", axis=1, tiled=True)
    piece_grad = lax.all_gather(recv_grad, "dp", axis=1, tiled=True)
    hidden, hidden_grad = expert_rows(piece_x, piece_grad, w_up, w_down)
    grad_in = outer_in(piece_x, hidden_grad)
    grad_out = outer_out(hidden, piece_grad)
    absorb_hidden_all = jnp.swapaxes(hidden, 0, 1)
    hidden_all, grad_in, grad_out = (absorb_hidden_all, grad_in, grad_out)
    summed = lax.psum_scatter(
        jnp.einsum("rkf,kfd->rkd", hidden_all, w_down, preferred_element_type=jnp.float32).astype(
            jnp.bfloat16
        ),
        "dp",
        scatter_dimension=0,
        tiled=True,
    )
    outgoing = jnp.swapaxes(summed, 0, 1).reshape(local_count, holders, capacity, width)
    returned = lax.all_to_all(outgoing, "expert", split_axis=1, concat_axis=1, tiled=True)
    expert_out = jnp.take(returned.reshape(slot_count, width), slots, axis=0)
    field = tokens.astype(jnp.float32) + expert_out.astype(jnp.float32)
    logits = jnp.dot(
        field, w_head, precision=lax.Precision.HIGHEST, preferred_element_type=jnp.float32
    )
    positive = jax.nn.softplus(logits) + 0.1
    fine_precip = mass[:, None] * positive / jnp.sum(positive, axis=1, keepdims=True)
    up_next, up_moment_next, up_square_next = adam_step(w_up, up_moment, up_square, grad_in)
    down_next, down_moment_next, down_square_next = adam_step(
        w_down, down_moment, down_square, grad_out
    )
    return (
        fine_precip,
        up_next,
        down_next,
        up_moment_next,
        up_square_next,
        down_moment_next,
        down_square_next,
    )


def solution(mesh):
    placed = (
        P(("dp", "expert"), None),
        P(("dp", "expert"), None),
        P(("dp", "expert"), None),
        P(),
        P(("dp", "expert")),
        P(),
        P("expert", None, "dp"),
        P("expert", "dp", None),
        P("expert", None, "dp"),
        P("expert", None, "dp"),
        P("expert", "dp", None),
        P("expert", "dp", None),
    )
    return jax.shard_map(
        local,
        mesh=mesh,
        in_specs=placed,
        out_specs=(
            P(("dp", "expert"), None),
            P("expert", None, "dp"),
            P("expert", "dp", None),
            P("expert", None, "dp"),
            P("expert", None, "dp"),
            P("expert", "dp", None),
            P("expert", "dp", None),
        ),
        check_vma=False,
    )
```

profile of v0, /device:TPU:0, one launch (start us, length us, event | category | flops | bytes accessed | tf_op | source)
XLA Modules:
  0.0 84.9 jit_solution(13675732115365415259)
XLA Ops:
  7.2 0.8 select_reduce_fusion.2
  8.0 0.8 select_reduce_fusion.1
  9.3 1.0 %scatter_custom_fusion = s32[128]{0:T(128)S(1)} fusion(s32[128]{0:T(128)S(1)} %fusion.40, s32[128]{0:T(128)S(1)} %iota.12, s32[]{:T(128)} %constant.54.clone.1), kind=kCustom, calls=%fused_computation.83 | custom fusion | bytes 516 | tf_op jit(solution)/shard_map/scatter | solution.py:53
  10.3 0.9 %concatenate.6 = bf16[129,512]{1,0:T(8,128)(2,1)S(1)} pad(bf16[128,512]{1,0:T(8,128)(2,1)} %param.14, bf16[]{:T(256)} %constant.56.clone.1), padding=0_1x0_0 | pad | bytes 263170 | tf_op jit(solution)/shard_map/concatenate | solution.py:55
  11.2 0.9 %concatenate.7 = bf16[129,512]{1,0:T(8,128)(2,1)S(1)} pad(bf16[128,512]{1,0:T(8,128)(2,1)} %param.15, bf16[]{:T(256)} %constant.56.clone.1), padding=0_1x0_0 | pad | bytes 263170 | tf_op jit(solution)/shard_map/concatenate | solution.py:55
  12.1 0.8 gather_fusion.1
  13.0 0.8 gather_fusion.2
  14.0 0.7 copy.27
  14.7 7.4 %all-to-all-start = ((bf16[2,16,4,512]{3,2,0,1:T(4,128)(2,1)}), bf16[2,16,4,512]{3,2,0,1:T(4,128)(2,1)S(1)}, u32[]{:S(2)}, u32[]{:S(2)}) async-start(bf16[2,16,4,512]{3,2,0,1:T(4,128)(2,1)} %copy.27), calls=%async_computation | async-start | bytes 262144 | tf_op jit(solution)/shard_map/all_to_all | solution.py:103
  22.2 0.7 copy.31
  22.9 7.2 %all-to-all-done = bf16[2,16,4,512]{3,2,0,1:T(4,128)(2,1)S(1)} async-done(((bf16[2,16,4,512]{3,2,0,1:T(4,128)(2,1)}), bf16[2,16,4,512]{3,2,0,1:T(4,128)(2,1)S(1)}, u32[]{:S(2)}, u32[]{:S(2)}) %all-to-all-start) | async-done | bytes 131104 | tf_op jit(solution)/shard_map/all_to_all | solution.py:103
  30.0 3.5 %all-to-all-start.2 = ((bf16[2,16,4,512]{3,2,0,1:T(4,128)(2,1)}), bf16[2,16,4,512]{3,2,0,1:T(4,128)(2,1)S(1)}, u32[]{:S(2)}, u32[]{:S(2)}) async-start(bf16[2,16,4,512]{3,2,0,1:T(4,128)(2,1)} %copy.31), calls=%async_computation.3 | async-start | bytes 262144 | tf_op jit(solution)/shard_map/all_to_all | solution.py:104
  33.7 6.4 %all_gather.6 = bf16[2,128,512]{2,1,0:T(8,128)(2,1)S(1)} all-gather(bf16[2,64,512]{2,1,0:T(8,128)(2,1)S(1)} %reshape.142), channel_id=1, replica_groups=mesh['dp'=2,'expert'=16] {'dp'}, dimensions={1}, use_global_device_ids=true | all-gather | bytes 393216 | tf_op jit(solution)/shard_map/all_gather | solution.py:108
  40.1 1.4 %all-to-all-done.2 = bf16[2,16,4,512]{3,2,0,1:T(4,128)(2,1)S(1)} async-done(((bf16[2,16,4,512]{3,2,0,1:T(4,128)(2,1)}), bf16[2,16,4,512]{3,2,0,1:T(4,128)(2,1)S(1)}, u32[]{:S(2)}, u32[]{:S(2)}) %all-to-all-start.2) | async-done | bytes 131104 | tf_op jit(solution)/shard_map/all_to_all | solution.py:104
  41.5 5.9 %all_gather.7 = bf16[2,128,512]{2,1,0:T(8,128)(2,1)} all-gather(bf16[2,64,512]{2,1,0:T(8,128)(2,1)S(1)} %reshape.146), channel_id=1, replica_groups=mesh['dp'=2,'expert'=16] {'dp'}, dimensions={1}, use_global_device_ids=true | all-gather | bytes 393216 | tf_op jit(solution)/shard_map/all_gather | solution.py:109
  47.9 1.2 %fusion.8 = bf16[128,2,512]{2,0,1:T(8,128)(2,1)} fusion(bf16[2,1024,512]{2,1,0:T(8,128)(2,1)S(1)} %copy-done.2, f32[2,128,1024]{2,1,0:T(8,128)S(1)} %fusion.50), kind=kOutput, calls=%fused_computation.21 | convolution fusion | flops 269877248 | bytes 3407872 | tf_op jit(solution)/shard_map/rkf,kfd->rkd/dot_general | solution.py:116
  49.1 8.1 %fusion.5 = (bf16[2,512,1024]{2,1,0:T(8,128)(2,1)}, bf16[2,512,1024]{2,1,0:T(8,128)(2,1)}, bf16[2,512,1024]{2,1,0:T(8,128)(2,1)}) fusion(bf16[2,512,1024]{2,1,0:T(8,128)(2,1)} %param.23, bf16[2,512,1024]{2,1,0:T(8,128)(2,1)} %param.22, bf16[2,512,1024]{2,1,0:T(8,128)(2,1)S(1)} %copy-done.1, bf16[2,128,512]{2,1,0:T(8,128)(2,1)S(1)} %all_gather.6, ...), kind=kOutput, calls=%fused_computation.15 | convolution fusion | flops 559415296 | bytes 16252928 | tf_op jit(solution)/shard_map/krd,krf->kdf/dot_general | solution.py:69
  57.2 3.6 %reduce-scatter.2.cloned.1.call-done = bf16[64,2,512]{2,0,1:T(8,128)(2,1)} async-done(((bf16[128,2,512]{2,0,1:T(8,128)(2,1)}), bf16[64,2,512]{2,0,1:T(8,128)(2,1)}) %reduce-scatter.2.cloned.1.call-update) | async-done | bytes 131088 | tf_op jit(solution)/shard_map/reduce_scatter | solution.py:115
  60.8 0.9 %reshape.143 = bf16[2,16,4,512]{3,2,1,0:T(4,128)(2,1)S(1)} reshape(bf16[2,64,512]{2,1,0:T(8,128)(2,1)} %bitcast.47) | data formatting | bytes 262144 | tf_op jit(solution)/shard_map/reshape | solution.py:123
  61.7 0.7 copy.29
  62.4 5.6 %all-to-all-start.1 = ((bf16[2,16,4,512]{3,2,0,1:T(4,128)(2,1)}), bf16[2,16,4,512]{3,2,0,1:T(4,128)(2,1)S(1)}, u32[]{:S(2)}, u32[]{:S(2)}) async-start(bf16[2,16,4,512]{3,2,0,1:T(4,128)(2,1)} %copy.29), calls=%async_computation.2 | async-start | bytes 262144 | tf_op jit(solution)/shard_map/all_to_all | solution.py:124
  68.1 7.6 %fusion.4 = (bf16[2,1024,512]{2,1,0:T(8,128)(2,1)}, bf16[2,1024,512]{2,1,0:T(8,128)(2,1)}, bf16[2,1024,512]{2,1,0:T(8,128)(2,1)}) fusion(bf16[2,1024,512]{2,1,0:T(8,128)(2,1)} %param.25, bf16[2,1024,512]{2,1,0:T(8,128)(2,1)} %param.24, bf16[2,1024,512]{2,1,0:T(8,128)(2,1)} %param.21, bf16[2,128,512]{2,1,0:T(8,128)(2,1)} %all_gather.7, ...), kind=kOutput, calls=%fused_computation.14 | convolution fusion | flops 289669120 | bytes 13893632 | tf_op jit(solution)/shard_map/krf,krd->kfd/dot_general | solution.py:73
  76.1 0.8 gather_fusion
  77.4 0.6 multiply_divide_fusion
  (34 shorter events, 2.2 us)
Async XLA Ops:
  7.2 69.7 %copy-start = (f32[512,16]{0,1:T(8,128)S(1)}, f32[512,16]{0,1:T(8,128)}, u32[]{:S(2)}) copy-start(f32[512,16]{0,1:T(8,128)} %param.19) | copy-start | bytes 98308
  13.8 33.6 %copy-start.1 = (bf16[2,512,1024]{2,1,0:T(8,128)(2,1)S(1)}, bf16[2,512,1024]{2,1,0:T(8,128)(2,1)}, u32[]{:S(2)}) copy-start(bf16[2,512,1024]{2,1,0:T(8,128)(2,1)} %param.20) | copy-start | bytes 6291460
  14.7 15.3 %all-to-all-start = ((bf16[2,16,4,512]{3,2,0,1:T(4,128)(2,1)}), bf16[2,16,4,512]{3,2,0,1:T(4,128)(2,1)S(1)}, u32[]{:S(2)}, u32[]{:S(2)}) async-start(bf16[2,16,4,512]{3,2,0,1:T(4,128)(2,1)} %copy.27), calls=%async_computation | async-start | bytes 262144 | tf_op jit(solution)/shard_map/all_to_all | solution.py:103
  30.0 11.4 %all-to-all-start.2 = ((bf16[2,16,4,512]{3,2,0,1:T(4,128)(2,1)}), bf16[2,16,4,512]{3,2,0,1:T(4,128)(2,1)S(1)}, u32[]{:S(2)}, u32[]{:S(2)}) async-start(bf16[2,16,4,512]{3,2,0,1:T(4,128)(2,1)} %copy.31), calls=%async_computation.3 | async-start | bytes 262144 | tf_op jit(solution)/shard_map/all_to_all | solution.py:104
  33.5 27.2 %reduce-scatter.2.cloned.1.call-start = ((), (), s32[]{:S(2)}) async-start(), calls=%async_computation.4 | async-start | bytes 393216 | tf_op jit(solution)/shard_map/reduce_scatter | solution.py:115
  41.5 6.3 %copy-start.2 = (bf16[2,1024,512]{2,1,0:T(8,128)(2,1)S(1)}, bf16[2,1024,512]{2,1,0:T(8,128)(2,1)}, u32[]{:S(2)}) copy-start(bf16[2,1024,512]{2,1,0:T(8,128)(2,1)} %param.21) | copy-start | bytes 6291460
  62.4 13.5 %all-to-all-start.1 = ((bf16[2,16,4,512]{3,2,0,1:T(4,128)(2,1)}), bf16[2,16,4,512]{3,2,0,1:T(4,128)(2,1)S(1)}, u32[]{:S(2)}, u32[]{:S(2)}) async-start(bf16[2,16,4,512]{3,2,0,1:T(4,128)(2,1)} %copy.29), calls=%async_computation.2 | async-start | bytes 262144 | tf_op jit(solution)/shard_map/all_to_all | solution.py:124
  68.1 8.9 %copy-start.3 = (bf16[128,512]{1,0:T(8,128)(2,1)S(1)}, bf16[128,512]{1,0:T(8,128)(2,1)}, u32[]{:S(2)}) copy-start(bf16[128,512]{1,0:T(8,128)(2,1)} %param.14) | copy-start | bytes 393220
  68.1 9.3 %copy-start.4 = (f32[128]{0:T(128)S(1)}, f32[128]{0:T(128)}, u32[]{:S(2)}) copy-start(f32[128]{0:T(128)} %param.18) | copy-start | bytes 1540
Sparse Core Ops, SparseCore 0:
  49.2 11.5 reduce-scatter.1
where the time goes:
time: 85.4 us; the launch traced here: 84.9 us
  matrix products  17.8 us (21%)
  starting transfers between devices  16.6 us (19%)
  between operations  14.3 us (17%)
  waiting for transfers between devices  12.4 us (15%)
  blocking collectives  12.2 us (14%)
  local copies, waits for them, and re-layouts  8.77 us (10%)
  other arithmetic  2.8 us (3%)
    dot_general x1, matrix products, outer_in(): jnp.einsum('krd,krf->kdf', rows_x, hidden_grad, preferred_element_type=jn...  8.1 us
    dot_general x1, matrix products, outer_out(): jnp.einsum('krf,krd->kfd', hidden, rows_grad, preferred_element_type=jnp....  7.61 us
    all_to_all x1, starting transfers between devices, local(): lax.all_to_all(send_x, 'expert', split_axis=1, concat_axis=1, tiled=True)  7.41 us
    all_to_all x1, waiting for transfers between devices, local(): lax.all_to_all(send_x, 'expert', split_axis=1, concat_axis=1, tiled=True)  7.15 us
    all_gather x1, blocking collectives, local(): piece_x = lax.all_gather(recv_x, 'dp', axis=1, tiled=True)  6.35 us
    all_gather x1, blocking collectives, local(): piece_grad = lax.all_gather(recv_grad, 'dp', axis=1, tiled=True)  5.87 us
    all_to_all x1, starting transfers between devices, local(): lax.all_to_all(outgoing, 'expert', split_axis=1, concat_axis=1, tiled=True)  5.63 us
    reduce_scatter x1, waiting for transfers between devices, local(): lax.psum_scatter(jnp.einsum('rkf,kfd->rkd', hidden_all, w_down, preferred...  3.57 us
  transfers between devices with their start and end apart: 4, of which 4 were waited for; matrix products, arithmetic and copies ran while one was open for 20% of the time, Pallas kernels for 0%

commit v1 on v0

v1 whole, which is shorter than its diff:
```python
import functools
import math

import jax
import jax.numpy as jnp
from jax import lax
from jax.experimental import pallas as pl
from jax.experimental.pallas import tpu as pltpu
from jax.sharding import PartitionSpec as P

CAP = 4

beta_first = 0.9
beta_second = 0.95
correct_first = 1.0 - 0.9**20
correct_second = 1.0 - 0.95**20
learn_rate = 0.002
adam_epsilon = 1e-08

BF = jnp.bfloat16
F32 = jnp.float32
EXACT = lax.Precision.HIGHEST
VMEM = pl.BlockSpec(memory_space=pltpu.VMEM)
SMEM = pl.BlockSpec(memory_space=pltpu.SMEM)


def iota(shape, dim):
    return lax.broadcasted_iota(jnp.int32, shape, dim)


def dot(a, b, dims=((1,), (0,)), precision=None):
    return lax.dot_general(a, b, (dims, ((), ())), precision=precision, preferred_element_type=F32)


def gelu_parts(pre):
    normal_cdf = 0.5 * (1.0 + lax.erf(pre * 0.7071067811865476))
    density = jnp.exp(-0.5 * pre * pre) * 0.3989422804014327
    return (pre * normal_cdf, normal_cdf + pre * density)


def adam_step(weight, first, second, grad):
    new_first = beta_first * first.astype(F32) + (1.0 - beta_first) * grad
    new_second = beta_second * second.astype(F32) + ((1.0 - beta_second) * grad) * grad
    scaled = new_second * (1.0 / correct_second)
    root = scaled * lax.rsqrt(scaled) + adam_epsilon
    update = (new_first * (learn_rate / correct_first)) * lax.rsqrt(root * root)
    moved = weight.astype(F32) - update
    return (moved.astype(BF), new_first.astype(BF), new_second.astype(BF))


def pack_kernel(copies, labels, placement, tokens, cotangent, head, send, slot_out, own):
    experts = placement.shape[0]
    count, width = tokens.shape
    label = labels[...]
    regime = iota((experts, count), 0)
    held = jnp.zeros((experts, count), jnp.int32)
    for j in range(experts):
        held = jnp.where(regime == j, placement[j], held)
    chosen = held == label
    before = (iota((count, count), 0) < iota((count, count), 1)).astype(F32).astype(BF)
    earlier = dot(chosen.astype(F32).astype(BF), before)
    position = jnp.sum(jnp.where(chosen, earlier, 0.0), axis=0, keepdims=True).astype(jnp.int32)
    target = jnp.sum(jnp.where(chosen, regime, 0), axis=0, keepdims=True)
    slot = target * CAP + position
    slot_out[...] = slot
    rows = experts * CAP
    pick = (iota((rows, count), 0) == slot).astype(F32).astype(BF)
    x = dot(pick, tokens[...]).astype(BF)
    g = dot(pick, cotangent[...]).astype(BF)
    for part in range(copies):
        send[pl.ds(part * rows, rows), pl.ds(0, width)] = x
        send[pl.ds(part * rows, rows), pl.ds(width, width)] = g
    own[...] = dot(head[...], tokens[...].astype(F32), ((1,), (1,)), EXACT)


def unmix(local_count, expert, group):
    rows = group * CAP
    row = iota((rows, local_count * rows), 0)
    col = iota((rows, local_count * rows), 1)
    source = row // CAP * (local_count * CAP) + expert * CAP + row % CAP
    return (source == col).astype(F32).astype(BF)


def forward_kernel(local_count, group, recv, w_up, w_down, head, hidden, slope, part_out):
    expert = pl.program_id(0)
    width = w_up.shape[1]
    pixels = head.shape[0]
    lanes = local_count * CAP * pixels
    rows = group * CAP
    groups = recv.shape[0] // (rows * local_count)
    select = unmix(local_count, expert, group)
    lane = iota((rows, lanes), 1)
    mine = (lane // (CAP * pixels) == expert) & (
        lane // pixels % CAP == iota((rows, lanes), 0) % CAP
    )
    gather = (iota((group, rows), 1) // CAP == iota((group, rows), 0)).astype(F32)
    tiled_head = jnp.concatenate([head[...]] * (local_count * CAP), axis=0)

    def step(i, carry):
        span = rows * local_count
        mixed = recv[pl.ds(pl.multiple_of(i * span, span), span), pl.ds(0, width)]
        x = dot(select, mixed).astype(BF)
        value, slant = gelu_parts(dot(x, w_up[0]))
        value = value.astype(BF)
        hidden[0, pl.ds(pl.multiple_of(i * rows, rows), rows), :] = value
        slope[0, pl.ds(pl.multiple_of(i * rows, rows), rows), :] = slant
        out = dot(value, w_down[0]).astype(BF)
        logit = dot(out.astype(F32), tiled_head, ((1,), (1,)), EXACT)
        logit = dot(gather, jnp.where(mine, logit, 0.0), precision=EXACT)
        here = pl.ds(pl.multiple_of(i * group, group), group)

        @pl.when(expert == 0)
        def _():
            part_out[here, :] = logit

        @pl.when(expert > 0)
        def _():
            part_out[here, :] += logit

        return carry

    if groups == 1:
        step(0, 0)
    else:
        lax.fori_loop(0, groups, step, 0)


def update_kernel(
    local_count,
    group,
    recv,
    hidden,
    slope,
    w_up,
    w_down,
    up_m,
    up_v,
    down_m,
    down_v,
    up_next,
    down_next,
    up_m_next,
    up_v_next,
    down_m_next,
    down_v_next,
    x_t,
    g_all,
):
    expert = pl.program_id(0)
    width = w_up.shape[1]
    chunk = w_up.shape[2]
    rows = group * CAP
    span = rows * local_count
    groups = recv.shape[0] // span

    @pl.when(pl.program_id(1) == 0)
    def _():
        select = unmix(local_count, expert, group)

        def step(i, carry):
            mixed = recv[pl.ds(pl.multiple_of(i * span, span), span), :]
            both = dot(select, mixed)
            here = pl.ds(pl.multiple_of(i * rows, rows), rows)
            x_t[:, here] = both[:, :width].T.astype(BF)
            g_all[here, :] = both[:, width:].astype(BF)
            return carry

        if groups == 1:
            step(0, 0)
        else:
            lax.fori_loop(0, groups, step, 0)

    g = g_all[...]
    back = dot(g, w_down[0], ((1,), (1,)))
    hidden_grad = (back * slope[0]).astype(BF)
    hidden_t = hidden[0].T
    tile = min(64, chunk)
    for start in range(0, width, tile):
        here = pl.ds(start, tile)
        grad = dot(x_t[here, :], hidden_grad)
        w, m, v = adam_step(w_up[0, here, :], up_m[0, here, :], up_v[0, here, :], grad)
        up_next[0, here, :] = w
        up_m_next[0, here, :] = m
        up_v_next[0, here, :] = v
    tile = min(32, chunk)
    for start in range(0, chunk, tile):
        here = pl.ds(start, tile)
        grad = dot(hidden_t[start : start + tile, :], g)
        w, m, v = adam_step(w_down[0, here, :], down_m[0, here, :], down_v[0, here, :], grad)
        down_next[0, here, :] = w
        down_m_next[0, here, :] = m
        down_v_next[0, here, :] = v


def finish_kernel(holders, slot, returned, own, mass, out):
    pixels, count = own.shape
    lanes = returned.shape[1]
    copies = returned.shape[0] // holders
    total = returned[pl.ds(0, holders), :]
    for part in range(1, copies):
        total = total + returned[pl.ds(part * holders, holders), :]
    places = lanes // pixels
    holder = slot[...] // places
    place = slot[...] % places
    pick = (iota((holders, count), 0) == holder).astype(F32)
    spread = dot(total, pick, ((0,), (0,)), EXACT)
    logits = own[...]
    for q in range(places):
        logits = logits + jnp.where(place == q, spread[q * pixels : (q + 1) * pixels, :], 0.0)
    positive = jax.nn.softplus(logits) + 0.1
    out[...] = mass[...] * positive / jnp.sum(positive, axis=0, keepdims=True)


def shape(*args):
    return jax.ShapeDtypeStruct(*args)


def local(
    tokens,
    cotangent,
    labels,
    placement,
    mass,
    w_head,
    w_up,
    w_down,
    up_moment,
    up_square,
    down_moment,
    down_square,
):
    experts = placement.shape[0]
    count, width = tokens.shape
    pixels = w_head.shape[1]
    local_count, _, hidden_count = w_up.shape
    holders = lax.axis_size("expert")
    copies = lax.axis_size("dp")
    sources = holders * copies
    group = math.gcd(sources, 32)
    lanes = local_count * CAP * pixels
    rows = sources * CAP
    mixed_rows = rows * local_count
    head = w_head.T
    axes = ("dp", "expert")

    send, slot, own = pl.pallas_call(
        functools.partial(pack_kernel, copies),
        out_shape=(
            shape((copies * experts * CAP, 2 * width), BF),
            shape((1, count), jnp.int32),
            shape((pixels, count), F32),
        ),
        in_specs=[VMEM, SMEM, VMEM, VMEM, VMEM],
        out_specs=(VMEM, VMEM, VMEM),
        name="pack",
    )(labels.reshape(1, count), placement, tokens, cotangent, head)

    recv = lax.all_to_all(send, axes, split_axis=0, concat_axis=0, tiled=True)

    hidden, slope, part_out = pl.pallas_call(
        functools.partial(forward_kernel, local_count, group),
        grid=(local_count,),
        out_shape=(
            shape((local_count, rows, hidden_count), BF),
            shape((local_count, rows, hidden_count), F32),
            shape((sources, lanes), F32),
        ),
        in_specs=[
            pl.BlockSpec((mixed_rows, width), lambda k: (0, 0)),
            pl.BlockSpec((1, width, hidden_count), lambda k: (k, 0, 0)),
            pl.BlockSpec((1, hidden_count, width), lambda k: (k, 0, 0)),
            pl.BlockSpec((pixels, width), lambda k: (0, 0)),
        ],
        out_specs=(
            pl.BlockSpec((1, rows, hidden_count), lambda k: (k, 0, 0)),
            pl.BlockSpec((1, rows, hidden_count), lambda k: (k, 0, 0)),
            pl.BlockSpec((sources, lanes), lambda k: (0, 0)),
        ),
        name="forward",
    )(recv, w_up, w_down, head)

    returned = lax.all_to_all(
        part_out.reshape(sources, 1, lanes), axes, split_axis=0, concat_axis=0, tiled=True
    ).reshape(sources, lanes)

    chunk = math.gcd(hidden_count, 256)
    up_block = pl.BlockSpec((1, width, chunk), lambda k, f: (k, 0, f))
    down_block = pl.BlockSpec((1, chunk, width), lambda k, f: (k, f, 0))
    row_block = pl.BlockSpec((1, rows, chunk), lambda k, f: (k, 0, f))
    up_shape = shape(w_up.shape, BF)
    down_shape = shape(w_down.shape, BF)
    updates = pl.pallas_call(
        functools.partial(update_kernel, local_count, group),
        grid=(local_count, hidden_count // chunk),
        out_shape=(up_shape, down_shape, up_shape, up_shape, down_shape, down_shape),
        in_specs=[
            pl.BlockSpec((mixed_rows, 2 * width), lambda k, f: (0, 0)),
            row_block,
            row_block,
            up_block,
            down_block,
            up_block,
            up_block,
            down_block,
            down_block,
        ],
        out_specs=(up_block, down_block, up_block, up_block, down_block, down_block),
        scratch_shapes=[pltpu.VMEM((width, rows), BF), pltpu.VMEM((rows, width), BF)],
        cost_estimate=pl.CostEstimate(
            flops=6 * rows * width * hidden_count * local_count,
            bytes_accessed=24 * width * hidden_count * local_count,
            transcendentals=0,
        ),
        name="update",
    )(recv, hidden, slope, w_up, w_down, up_moment, up_square, down_moment, down_square)

    fine = pl.pallas_call(
        functools.partial(finish_kernel, holders),
        out_shape=shape((pixels, count), F32),
        in_specs=[VMEM] * 4,
        out_specs=VMEM,
        name="finish",
    )(slot, returned, own, mass.reshape(1, count))
    return (fine.T,) + tuple(updates)


def solution(mesh):
    tokens = P(("dp", "expert"), None)
    up = P("expert", None, "dp")
    down = P("expert", "dp", None)
    return jax.shard_map(
        local,
        mesh=mesh,
        in_specs=(tokens, tokens, tokens, P(), P(("dp", "expert")), P())
        + (up, down, up, up, down, down),
        out_specs=(tokens, up, down, up, up, down, down),
        check_vma=False,
    )
```

time: 85.4 us -> 51.6 us (0.60)
  Pallas kernels: 0 us -> 24.1 us
  matrix products: 17.8 us -> 0 us
  starting transfers between devices: 16.6 us -> 2.5 us
  between operations: 14.3 us -> 0.67 us
  waiting for transfers between devices: 12.4 us -> 0.01 us
  blocking collectives: 12.2 us -> 23.3 us
  local copies, waits for them, and re-layouts: 8.77 us -> 0.59 us
  other arithmetic: 2.8 us -> 0 us
    pallas_call x0 -> x4, Pallas kernels: none -> 24.1 us  [the longest x1 15.1 us: local(): pl.pallas_call(functools.partial(update_kernel, local_count, group), grid...]
    all_to_all x0 -> x1, blocking collectives: none -> 23.3 us  [local(): recv = lax.all_to_all(send, axes, split_axis=0, concat_axis=0, tiled=True)]
    dot_general x5 -> x0, matrix products: 17.8 us -> none  [the longest x1 8.1 us: outer_in(): jnp.einsum('krd,krf->kdf', rows_x, hidden_grad, preferred_element_type=jn...]
    all_to_all x3 -> x1, starting transfers between devices: 16.6 us -> 2.5 us  [local(): lax.all_to_all(part_out.reshape(sources, 1, lanes), axes, split_axis=0, c...]
    all_gather x2 -> x0, blocking collectives: 12.2 us -> none  [the longest x1 6.35 us: local(): piece_x = lax.all_gather(recv_x, 'dp', axis=1, tiled=True)]
    all_to_all x3 -> x1, waiting for transfers between devices: 8.77 us -> 0.01 us  [local(): lax.all_to_all(part_out.reshape(sources, 1, lanes), axes, split_axis=0, c...]
    reduce_scatter x1 -> x0, waiting for transfers between devices: 3.57 us -> none  [local(): lax.psum_scatter(jnp.einsum('rkf,kfd->rkd', hidden_all, w_down, preferred...]
    reshape x9 -> x0, local copies, waits for them, and re-layouts: 3.24 us -> none  [the longest x2 1.65 us: local(): jnp.swapaxes(summed, 0, 1).reshape(local_count, holders, capacity, width)]
  transfers between devices with their start and end apart: 4 -> 1, of which waited for: 4 -> 0; matrix products, arithmetic and copies ran while one was open for 20% -> 0% of each run, Pallas kernels for 0% -> 29%
where the time goes in v1:
time: 51.6 us; the launch traced here: 51.2 us
  Pallas kernels  24.1 us (47%)
  blocking collectives  23.3 us (45%)
  starting transfers between devices  2.5 us (5%)
  between operations  0.67 us (1%)
  local copies, waits for them, and re-layouts  0.59 us (1%)
    all_to_all x1, blocking collectives, local(): recv = lax.all_to_all(send, axes, split_axis=0, concat_axis=0, tiled=True)  23.3 us
    pallas_call x1, Pallas kernels, local(): pl.pallas_call(functools.partial(update_kernel, local_count, group), grid...  15.1 us
    pallas_call x1, Pallas kernels, local(): pl.pallas_call(functools.partial(forward_kernel, local_count, group), gri...  5.23 us
    all_to_all x1, starting transfers between devices, local(): lax.all_to_all(part_out.reshape(sources, 1, lanes), axes, split_axis=0, c...  2.5 us
    pallas_call x1, Pallas kernels, local(): pl.pallas_call(functools.partial(pack_kernel, copies), out_shape=(shape((...  2.2 us
    pallas_call x1, Pallas kernels, local(): pl.pallas_call(functools.partial(finish_kernel, holders), out_shape=shape...  1.62 us
  transfers between devices with their start and end apart: 1, of which 0 were waited for; matrix products, arithmetic and copies ran while one was open for 0% of the time, Pallas kernels for 29%

profile of v1, /device:TPU:0, one launch (start us, length us, event | category | flops | bytes accessed | tf_op | source)
XLA Modules:
  0.0 51.2 jit_solution(6152882703734023019)
XLA Ops:
  0.6 2.2 %pack.1 = (bf16[256,1024]{1,0:T(8,128)(2,1)}, s32[1,128]{1,0:T(1,128)}, f32[16,128]{1,0:T(8,128)}) custom-call(s32[1,128]{1,0:T(1,128)} %bitcast.18, s32[32]{0:T(128)} %placement.1, bf16[128,512]{1,0:T(8,128)(2,1)} %tokens.1, bf16[128,512]{1,0:T(8,128)(2,1)} %cotangent.1, f32[16,512]{1,0:T(8,128)} %bitcast.13), custom_call_target="tpu_custom_call" | custom-call | tf_op jit(solution)/shard_map/pack/pallas_call | solution.py:246
  2.8 23.3 %all_to_all.16 = bf16[32,8,1024]{2,1,0:T(8,128)(2,1)} all-to-all(bf16[32,8,1024]{2,1,0:T(8,128)(2,1)} %bitcast.12), channel_id=1, replica_groups=mesh['dp'=2,'expert'=16] {'dp','expert'}, dimensions={0} | all-to-all | bytes 1048576 | tf_op jit(solution)/shard_map/all_to_all | solution.py:258
  26.1 5.2 %forward.1 = (bf16[2,128,1024]{2,1,0:T(8,128)(2,1)}, f32[2,128,1024]{2,1,0:T(8,128)}, f32[32,128]{1,0:T(8,128)}) custom-call(bf16[256,1024]{1,0:T(8,128)(2,1)} %bitcast.10, bf16[2,512,1024]{2,1,0:T(8,128)(2,1)} %w_up.3, bf16[2,1024,512]{2,1,0:T(8,128)(2,1)} %w_down.3, f32[16,512]{1,0:T(8,128)} %bitcast.14), custom_call_target="tpu_custom_call" | custom-call | tf_op jit(solution)/shard_map/forward/pallas_call | solution.py:260
  31.4 2.5 %all-to-all-start.1 = ((f32[32,1,128]{2,1,0:T(1,128)}), f32[32,1,128]{2,1,0:T(1,128)S(1)}, u32[]{:S(2)}, u32[]{:S(2)}) async-start(f32[32,1,128]{2,1,0:T(1,128)} %bitcast.16), calls=%async_computation.1 | async-start | bytes 32768 | tf_op jit(solution)/shard_map/all_to_all | solution.py:282
  33.9 15.1 %update.1 = (bf16[2,512,1024]{2,1,0:T(8,128)(2,1)}, bf16[2,1024,512]{2,1,0:T(8,128)(2,1)}, bf16[2,512,1024]{2,1,0:T(8,128)(2,1)}, bf16[2,512,1024]{2,1,0:T(8,128...) custom-call(bf16[256,1024]{1,0:T(8,128)(2,1)} %bitcast.11, ...), custom_call_target="tpu_custom_call" | custom-call | flops 805306368 | bytes 25165824 | tf_op jit(solution)/shard_map/update/pallas_call | solution.py:292
  49.0 0.0 all-to-all-done.1
  49.0 0.0 copy-start
  49.0 0.6 %copy-done = f32[32,1,128]{2,1,0:T(1,128)} copy-done((f32[32,1,128]{2,1,0:T(1,128)}, f32[32,1,128]{2,1,0:T(1,128)S(1)}, u32[]{:S(2)}) %copy-start) | copy-done | bytes 16408
  49.6 1.6 %finish.1 = f32[16,128]{1,0:T(8,128)} custom-call(s32[1,128]{1,0:T(1,128)} %get-tuple-element.19.slot, f32[32,128]{1,0:T(8,128)} %bitcast.15, f32[16,128]{1,0:T(8,128)} %get-tuple-element.22.own, f32[1,128]{1,0:T(1,128)} %bitcast.19), custom_call_target="tpu_custom_call" | custom-call | tf_op jit(solution)/shard_map/finish/pallas_call | solution.py:317
Async XLA Ops:
  31.4 17.6 %all-to-all-start.1 = ((f32[32,1,128]{2,1,0:T(1,128)}), f32[32,1,128]{2,1,0:T(1,128)S(1)}, u32[]{:S(2)}, u32[]{:S(2)}) async-start(f32[32,1,128]{2,1,0:T(1,128)} %bitcast.16), calls=%async_computation.1 | async-start | bytes 32768 | tf_op jit(solution)/shard_map/all_to_all | solution.py:282
  49.0 0.6 %copy-start = (f32[32,1,128]{2,1,0:T(1,128)}, f32[32,1,128]{2,1,0:T(1,128)S(1)}, u32[]{:S(2)}) copy-start(f32[32,1,128]{2,1,0:T(1,128)S(1)} %all-to-all-done.1) | copy-start | bytes 49156

commit v2 on v1

v2 whole, which is shorter than its diff:
```python
import functools
import math

import jax
import jax.numpy as jnp
from jax import lax
from jax.experimental import pallas as pl
from jax.experimental.pallas import tpu as pltpu
from jax.sharding import PartitionSpec as P

CAP = 4

beta_first = 0.9
beta_second = 0.95
correct_first = 1.0 - 0.9**20
correct_second = 1.0 - 0.95**20
learn_rate = 0.002
adam_epsilon = 1e-08

BF = jnp.bfloat16
F32 = jnp.float32
EXACT = lax.Precision.HIGHEST
VMEM = pl.BlockSpec(memory_space=pltpu.VMEM)
SMEM = pl.BlockSpec(memory_space=pltpu.SMEM)
HBM = pl.BlockSpec(memory_space=pltpu.HBM)


def iota(shape, dim):
    return lax.broadcasted_iota(jnp.int32, shape, dim)


def dot(a, b, dims=((1,), (0,)), precision=None):
    return lax.dot_general(a, b, (dims, ((), ())), precision=precision, preferred_element_type=F32)


def gelu_parts(pre):
    normal_cdf = 0.5 * (1.0 + lax.erf(pre * 0.7071067811865476))
    density = jnp.exp(-0.5 * pre * pre) * 0.3989422804014327
    return (pre * normal_cdf, normal_cdf + pre * density)


def adam_step(weight, first, second, grad):
    new_first = beta_first * first.astype(F32) + (1.0 - beta_first) * grad
    new_second = beta_second * second.astype(F32) + ((1.0 - beta_second) * grad) * grad
    scaled = new_second * (1.0 / correct_second)
    root = scaled * lax.rsqrt(scaled) + adam_epsilon
    update = (new_first * (learn_rate / correct_first)) * lax.rsqrt(root * root)
    moved = weight.astype(F32) - update
    return (moved.astype(BF), new_first.astype(BF), new_second.astype(BF))


def pack_kernel(labels, placement, tokens, cotangent, head, send, slot_out, own):
    experts = placement.shape[0]
    count, width = tokens.shape
    label = labels[...]
    regime = iota((experts, count), 0)
    held = jnp.zeros((experts, count), jnp.int32)
    for j in range(experts):
        held = jnp.where(regime == j, placement[j], held)
    chosen = held == label
    before = (iota((count, count), 0) < iota((count, count), 1)).astype(F32).astype(BF)
    earlier = dot(chosen.astype(F32).astype(BF), before)
    position = jnp.sum(jnp.where(chosen, earlier, 0.0), axis=0, keepdims=True).astype(jnp.int32)
    target = jnp.sum(jnp.where(chosen, regime, 0), axis=0, keepdims=True)
    slot = target * CAP + position
    slot_out[...] = slot
    pick = (iota((experts * CAP, count), 0) == slot).astype(F32).astype(BF)
    send[:, pl.ds(0, width)] = dot(pick, tokens[...]).astype(BF)
    send[:, pl.ds(width, width)] = dot(pick, cotangent[...]).astype(BF)
    own[...] = dot(head[...], tokens[...].astype(F32), ((1,), (1,)), EXACT)


def unmix(local_count, expert, rows):
    row = iota((rows, local_count * rows), 0)
    col = iota((rows, local_count * rows), 1)
    source = row // CAP * (local_count * CAP) + expert * CAP + row % CAP
    return (source == col).astype(F32).astype(BF)


def forward_rows(expert, mixed, w_up, w_down, tiled_head, pixels):
    local_count = w_up.shape[0]
    rows = mixed.shape[0] // local_count
    group = rows // CAP
    lanes = local_count * CAP * pixels
    x = dot(unmix(local_count, expert, rows), mixed).astype(BF)
    value, slant = gelu_parts(dot(x, w_up[expert]))
    value = value.astype(BF)
    out = dot(value, w_down[expert]).astype(BF)
    logit = dot(out.astype(F32), tiled_head, ((1,), (1,)), EXACT)
    lane = iota((rows, lanes), 1)
    mine = (lane // (CAP * pixels) == expert) & (
        lane // pixels % CAP == iota((rows, lanes), 0) % CAP
    )
    gather = (iota((group, rows), 1) // CAP == iota((group, rows), 0)).astype(F32)
    return value, slant, dot(gather, jnp.where(mine, logit, 0.0), precision=EXACT)


def own_kernel(recv, w_up, w_down, head, hidden, slope, part, up_here, down_here, sems):
    local_count, width, _ = w_up.shape
    copies = []
    for expert in range(local_count):
        for side, (there, here) in enumerate(((w_up, up_here), (w_down, down_here))):
            copy = pltpu.make_async_copy(
                there.at[expert], here.at[expert], sems.at[expert, side]
            )
            copy.start()
            copies.append(copy)
    tiled_head = jnp.concatenate([head[...]] * (local_count * CAP), axis=0)
    total = None
    for expert in range(local_count):
        copies[2 * expert].wait()
        copies[2 * expert + 1].wait()
        value, slant, logit = forward_rows(
            expert, recv[:, :width], up_here, down_here, tiled_head, head.shape[0]
        )
        hidden[expert] = value
        slope[expert] = slant
        total = logit if total is None else total + logit
    part[...] = total


def peer_kernel(copies, peers, w_up, w_down, head, part, hidden, slope, out):
    local_count = w_up.shape[0]
    span = peers.shape[0] // (copies - 1)
    rows = span // local_count
    group = rows // CAP
    here = lax.axis_index("dp")
    tiled_head = jnp.concatenate([head[...]] * (local_count * CAP), axis=0)
    out[pl.ds(pl.multiple_of(here * group, 8), group), :] = part[...]
    for step in range(1, copies):
        total = None
        for expert in range(local_count):
            value, slant, logit = forward_rows(
                expert,
                peers[pl.ds((step - 1) * span, span), :],
                w_up,
                w_down,
                tiled_head,
                head.shape[0],
            )
            hidden[expert, pl.ds((step - 1) * rows, rows), :] = value
            slope[expert, pl.ds((step - 1) * rows, rows), :] = slant
            total = logit if total is None else total + logit
        owner = lax.rem(here - step + copies, copies)
        out[pl.ds(pl.multiple_of(owner * group, 8), group), :] = total


def update_kernel(
    copies,
    recv,
    peer_x,
    peer_g,
    hidden_own,
    hidden_peer,
    slope_own,
    slope_peer,
    w_up,
    w_down,
    up_m,
    up_v,
    down_m,
    down_v,
    up_next,
    down_next,
    up_m_next,
    up_v_next,
    down_m_next,
    down_v_next,
    ups,
    downs,
    x_t,
    g_all,
    hidden_grad,
    hidden_t,
    sems,
):
    local_count, width, hidden_count = w_up.shape
    up_tile = math.gcd(width, 128)
    down_tile = math.gcd(hidden_count, 256)
    up_steps = width // up_tile
    down_steps = hidden_count // down_tile
    steps = up_steps + down_steps
    span = recv.shape[0]
    rows = span // local_count

    def moves(expert, step, down, out):
        tile = down_tile if down else up_tile
        held = downs if down else ups
        pairs = (
            ((w_down, down_next), (down_m, down_m_next), (down_v, down_v_next))
            if down
            else ((w_up, up_next), (up_m, up_m_next), (up_v, up_v_next))
        )
        number = expert * steps + step + (0 if down else down_steps)
        here = pl.ds(pl.multiple_of(step * tile, tile), tile)
        return [
            pltpu.make_async_copy(
                held.at[i, expert, here] if out else pair[0].at[expert, here],
                pair[1].at[expert, here] if out else held.at[i, expert, here],
                sems.at[int(out), number, i],
            )
            for i, pair in enumerate(pairs)
        ]

    def every(action, out):
        def expert_loop(expert, carry):
            for down, count in ((True, down_steps), (False, up_steps)):

                def step_loop(step, carry, down=down):
                    for move in moves(expert, step, down, out):
                        action(move)
                    return carry

                lax.fori_loop(0, count, step_loop, 0)
            return carry

        lax.fori_loop(0, local_count, expert_loop, 0)

    every(lambda move: move.start(), False)

    def expert_loop(expert, carry):
        select = unmix(local_count, expert, rows)
        for step in range(copies):
            if step == 0:
                x, g = recv[:, :width], recv[:, width:]
            else:
                x = peer_x[pl.ds((step - 1) * span, span), :]
                g = peer_g[pl.ds((step - 1) * span, span), :]
            here = pl.ds(step * rows, rows)
            x_t[:, here] = dot(select, x).T.astype(BF)
            g_all[here, :] = dot(select, g).astype(BF)
        hidden_t[:, pl.ds(0, rows)] = hidden_own[expert].T
        hidden_t[:, pl.ds(rows, rows * (copies - 1))] = hidden_peer[expert].T

        def down_loop(step, carry):
            for move in moves(expert, step, True, False):
                move.wait()
            here = pl.ds(pl.multiple_of(step * down_tile, down_tile), down_tile)
            back = dot(g_all[...], downs[0, expert, here], ((1,), (1,)))
            hidden_grad[pl.ds(0, rows), here] = (
                back[:rows] * slope_own[expert, :, here]
            ).astype(BF)
            hidden_grad[pl.ds(rows, rows * (copies - 1)), here] = (
                back[rows:] * slope_peer[expert, :, here]
            ).astype(BF)
            tile = math.gcd(down_tile, 32)
            for start in range(0, down_tile, tile):
                at = pl.ds(pl.multiple_of(step * down_tile + start, tile), tile)
                grad = dot(hidden_t[at, :], g_all[...])
                new = adam_step(*[downs[i, expert, at] for i in range(3)], grad)
                for i in range(3):
                    downs[i, expert, at] = new[i]
            for move in moves(expert, step, True, True):
                move.start()
            return carry

        lax.fori_loop(0, down_steps, down_loop, 0)

        def up_loop(step, carry):
            for move in moves(expert, step, False, False):
                move.wait()
            tile = math.gcd(up_tile, 16)
            for start in range(0, up_tile, tile):
                at = pl.ds(pl.multiple_of(step * up_tile + start, tile), tile)
                grad = dot(x_t[at, :], hidden_grad[...])
                new = adam_step(*[ups[i, expert, at] for i in range(3)], grad)
                for i in range(3):
                    ups[i, expert, at] = new[i]
            for move in moves(expert, step, False, True):
                move.start()
            return carry

        lax.fori_loop(0, up_steps, up_loop, 0)
        return carry

    lax.fori_loop(0, local_count, expert_loop, 0)
    every(lambda move: move.wait(), True)


def finish_kernel(holders, slot, returned, own, mass, out):
    pixels, count = own.shape
    lanes = returned.shape[1]
    copies = returned.shape[0] // holders
    total = returned[pl.ds(0, holders), :]
    for part in range(1, copies):
        total = total + returned[pl.ds(part * holders, holders), :]
    places = lanes // pixels
    holder = slot[...] // places
    place = slot[...] % places
    pick = (iota((holders, count), 0) == holder).astype(F32)
    spread = dot(total, pick, ((0,), (0,)), EXACT)
    logits = own[...]
    for q in range(places):
        logits = logits + jnp.where(place == q, spread[q * pixels : (q + 1) * pixels, :], 0.0)
    positive = jax.nn.softplus(logits) + 0.1
    out[...] = mass[...] * positive / jnp.sum(positive, axis=0, keepdims=True)


def shape(*args):
    return jax.ShapeDtypeStruct(*args)


def stay(value):
    return pltpu.with_memory_space_constraint(value, pltpu.HBM)


def limit(mib):
    return pltpu.CompilerParams(vmem_limit_bytes=mib << 20)


def local(
    tokens,
    cotangent,
    labels,
    placement,
    mass,
    w_head,
    w_up,
    w_down,
    up_moment,
    up_square,
    down_moment,
    down_square,
):
    w_up, w_down, up_moment, up_square, down_moment, down_square = [
        stay(value) for value in (w_up, w_down, up_moment, up_square, down_moment, down_square)
    ]
    experts = placement.shape[0]
    count, width = tokens.shape
    pixels = w_head.shape[1]
    local_count, _, hidden_count = w_up.shape
    holders = lax.axis_size("expert")
    copies = lax.axis_size("dp")
    sources = holders * copies
    lanes = local_count * CAP * pixels
    rows = holders * CAP
    head = w_head.T
    up_shape = shape(w_up.shape, BF)
    down_shape = shape(w_down.shape, BF)
    one_product = 2 * rows * width * hidden_count * local_count

    send, slot, own = pl.pallas_call(
        pack_kernel,
        out_shape=(
            shape((experts * CAP, 2 * width), BF),
            shape((1, count), jnp.int32),
            shape((pixels, count), F32),
        ),
        in_specs=[VMEM, SMEM, VMEM, VMEM, VMEM],
        out_specs=(VMEM, VMEM, VMEM),
        compiler_params=limit(4),
        name="pack",
    )(stay(labels.reshape(1, count)), stay(placement), stay(tokens), stay(cotangent), stay(head))

    recv = lax.all_to_all(send, "expert", split_axis=0, concat_axis=0, tiled=True)

    def to_peers(value):
        moved = [
            lax.ppermute(value, "dp", [(i, (i + step) % copies) for i in range(copies)])
            for step in range(1, copies)
        ]
        return moved[0] if copies == 2 else jnp.concatenate(moved, axis=0)

    peer_x = to_peers(recv[:, :width])
    peer_g = to_peers(recv[:, width:])

    hidden_own, slope_own, part, up_here, down_here = pl.pallas_call(
        own_kernel,
        out_shape=(
            shape((local_count, rows, hidden_count), BF),
            shape((local_count, rows, hidden_count), F32),
            shape((holders, lanes), F32),
            pltpu.VMEM(w_up.shape, BF),
            pltpu.VMEM(w_down.shape, BF),
        ),
        in_specs=[VMEM, HBM, HBM, VMEM],
        out_specs=(VMEM,) * 5,
        scratch_shapes=[pltpu.SemaphoreType.DMA((local_count, 2))],
        compiler_params=limit(16),
        cost_estimate=pl.CostEstimate(
            flops=4 * one_product, bytes_accessed=4 * width * hidden_count * local_count, transcendentals=0
        ),
        name="own_rows",
    )(recv, w_up, w_down, stay(head))

    hidden_peer, slope_peer, scores = pl.pallas_call(
        functools.partial(peer_kernel, copies),
        out_shape=(
            shape((local_count, rows * (copies - 1), hidden_count), BF),
            shape((local_count, rows * (copies - 1), hidden_count), F32),
            shape((sources, lanes), F32),
        ),
        in_specs=[VMEM] * 5,
        out_specs=(VMEM,) * 3,
        compiler_params=limit(16),
        cost_estimate=pl.CostEstimate(
            flops=2 * one_product, bytes_accessed=0, transcendentals=0
        ),
        name="peer_rows",
    )(peer_x, up_here, down_here, stay(head), part)

    returned = lax.all_to_all(
        scores.reshape(sources, 1, lanes),
        ("dp", "expert"),
        split_axis=0,
        concat_axis=0,
        tiled=True,
    ).reshape(sources, lanes)

    steps = width // math.gcd(width, 128) + hidden_count // math.gcd(hidden_count, 256)
    updates = pl.pallas_call(
        functools.partial(update_kernel, copies),
        out_shape=(up_shape, down_shape, up_shape, up_shape, down_shape, down_shape),
        in_specs=[VMEM] * 7 + [HBM] * 6,
        out_specs=(HBM,) * 6,
        scratch_shapes=[
            pltpu.VMEM((3,) + w_up.shape, BF),
            pltpu.VMEM((3,) + w_down.shape, BF),
            pltpu.VMEM((width, rows * copies), BF),
            pltpu.VMEM((rows * copies, width), BF),
            pltpu.VMEM((rows * copies, hidden_count), BF),
            pltpu.VMEM((hidden_count, rows * copies), BF),
            pltpu.SemaphoreType.DMA((2, local_count * steps, 3)),
        ],
        compiler_params=limit(24),
        cost_estimate=pl.CostEstimate(
            flops=6 * one_product * copies,
            bytes_accessed=24 * width * hidden_count * local_count,
            transcendentals=0,
        ),
        name="update",
    )(
        recv,
        peer_x,
        peer_g,
        hidden_own,
        hidden_peer,
        slope_own,
        slope_peer,
        w_up,
        w_down,
        up_moment,
        up_square,
        down_moment,
        down_square,
    )

    fine = pl.pallas_call(
        functools.partial(finish_kernel, holders),
        out_shape=shape((pixels, count), F32),
        in_specs=[VMEM] * 4,
        out_specs=VMEM,
        compiler_params=limit(2),
        name="finish",
    )(slot, returned, own, stay(mass.reshape(1, count)))
    return (fine.T,) + tuple(updates)


def solution(mesh):
    tokens = P(("dp", "expert"), None)
    up = P("expert", None, "dp")
    down = P("expert", "dp", None)
    return jax.shard_map(
        local,
        mesh=mesh,
        in_specs=(tokens, tokens, tokens, P(), P(("dp", "expert")), P())
        + (up, down, up, up, down, down),
        out_specs=(tokens, up, down, up, up, down, down),
        check_vma=False,
    )
```

time: 51.6 us -> 47 us (0.911)
  blocking collectives: 23.3 us -> 17.2 us
  starting transfers between devices: 2.5 us -> 4.88 us
  local copies, waits for them, and re-layouts: 0.59 us -> 0.02 us
    all_to_all x1, blocking collectives: 23.3 us -> 17.2 us  [local(): lax.all_to_all(send, 'expert', split_axis=0, concat_axis=0, tiled=True)]
    ppermute x0 -> x2, starting transfers between devices: none -> 2.09 us  [to_peers(): lax.ppermute(value, 'dp', [(i, (i + step) % copies) for i in range(copies)])]
    unnamed x2 -> x0, local copies, waits for them, and re-layouts: 0.59 us -> none
    pallas_call x3 -> x4, Pallas kernels: 22.5 us -> 22.3 us  [the longest x1 12.6 us: local(): pl.pallas_call(functools.partial(update_kernel, copies), out_shape=(up_sh...]
  transfers between devices with their start and end apart: 1 -> 3, of which waited for: 0 -> 0; matrix products, arithmetic and copies ran while one was open for 0% -> 0% of each run, Pallas kernels for 29% -> 45%
where the time goes in v2:
time: 47 us; the launch traced here: 46.7 us
  Pallas kernels  23.9 us (51%)
  blocking collectives  17.2 us (37%)
  starting transfers between devices  4.88 us (10%)
  between operations  0.69 us (1%)
    all_to_all x1, blocking collectives, local(): lax.all_to_all(send, 'expert', split_axis=0, concat_axis=0, tiled=True)  17.2 us
    pallas_call x1, Pallas kernels, local(): pl.pallas_call(functools.partial(update_kernel, copies), out_shape=(up_sh...  12.6 us
    pallas_call x1, Pallas kernels, local(): pl.pallas_call(own_kernel, out_shape=(shape((local_count, rows, hidden_co...  4.93 us
    pallas_call x1, Pallas kernels, local(): pl.pallas_call(functools.partial(peer_kernel, copies), out_shape=(shape((...  3.29 us
    all_to_all x1, starting transfers between devices, local(): lax.all_to_all(scores.reshape(sources, 1, lanes), ('dp', 'expert'), split...  2.79 us
    ppermute x2, starting transfers between devices, to_peers(): lax.ppermute(value, 'dp', [(i, (i + step) % copies) for i in range(copies)])  2.09 us
    pallas_call x1, Pallas kernels, local(): pl.pallas_call(functools.partial(finish_kernel, holders), out_shape=shape...  1.55 us
    pallas_call x1, Pallas kernels, local(): pl.pallas_call(pack_kernel, out_shape=(shape((experts * CAP, 2 * width),...  1.5 us
  transfers between devices with their start and end apart: 3, of which 0 were waited for; matrix products, arithmetic and copies ran while one was open for 0% of the time, Pallas kernels for 45%

profile of v2, /device:TPU:0, one launch (start us, length us, event | category | flops | bytes accessed | tf_op | source)
XLA Modules:
  0.0 46.7 jit_solution(14731207233512850310)
XLA Ops:
  0.6 1.5 %pack.1 = (bf16[128,1024]{1,0:T(8,128)(2,1)S(1)}, s32[1,128]{1,0:T(1,128)S(1)}, f32[16,128]{1,0:T(8,128)S(1)}) custom-call(s32[1,128]{1,0:T(1,128)} %bitcast.19, s32[32]{0:T(128)} %placement.1, bf16[128,512]{1,0:T(8,128)(2,1)} %tokens.1, bf16[128,512]{1,0:T(8,128)(2,1)} %cotangent.1, f32[16,512]{1,0:T(8,128)} %bitcast.15), custom_call_target="tpu_custom_call" | custom-call | tf_op jit(solution)/shard_map/pack/pallas_call | solution.py:342
  2.1 17.2 %all_to_all.16 = bf16[16,8,1024]{2,1,0:T(8,128)(2,1)S(1)} all-to-all(bf16[16,8,1024]{2,1,0:T(8,128)(2,1)S(1)} %bitcast.13), channel_id=1, replica_groups=mesh['dp'=2,'expert'=16] {'expert'}, dimensions={0} | all-to-all | bytes 524288 | tf_op jit(solution)/shard_map/all_to_all | solution.py:355
  19.4 1.6 %collective-permute-start = (bf16[128,512]{1,0:T(8,128)(2,1)S(1)}, bf16[128,512]{1,0:T(8,128)(2,1)S(1)}, u32[]{:S(2)}, u32[]{:S(2)}) collective-permute-start(bf16[128,512]{1,0:T(8,128)(2,1)S(1)} %get-tuple-element.42), channel_id=1, source_target_pairs={{0,16},{16,0},{1,17},{17,1},{2,18},{18,2},{3,19},{19,3},{4,20},{20... | collective-permute-start | bytes 393224 | tf_op jit(solution)/shard_map/ppermute | solution.py:359
  20.9 0.5 %collective-permute-start.1 = (bf16[128,512]{1,0:T(8,128)(2,1)S(1)}, bf16[128,512]{1,0:T(8,128)(2,1)S(1)}, u32[]{:S(2)}, u32[]{:S(2)}) collective-permute-start(bf16[128,512]{1,0:T(8,128)(2,1)S(1)} %get-tuple-element.41), channel_id=1, source_target_pairs={{0,16},{16,0},{1,17},{17,1},{2,18},{18,2},{3,19},{19,3},{4,20},{20... | collective-permute-start | bytes 393224 | tf_op jit(solution)/shard_map/ppermute | solution.py:359
  21.5 4.9 %own_rows.1 = (bf16[2,64,1024]{2,1,0:T(8,128)(2,1)S(1)}, f32[2,64,1024]{2,1,0:T(8,128)S(1)}, f32[16,128]{1,0:T(8,128)S(1)}, bf16[2,512,1024]{2,1,0:T(8,128)(2,1)S(1)}, bf16[2,1024,512]{2,1,0:T(8,128)(2,1)S(1)}) custom-call(bf16[128,1024]{1,0:T(8,128)(2,1)S(1)} %bitcast.11, bf16[2,512,1024]{2,1,0:T(8,128)(2,1)} %w_up.3, bf16[2,1024,512]{2,1,0:T(8,128)(2,1)} %w_down.3, ...), custom_call_target="tpu_custom_call" | custom-call | flops 536870912 | bytes 4194304 | tf_op jit(solution)/shard_map/own_rows/pallas_call | solution.py:367
  26.4 0.0 collective-permute-done.peers.peer_x
  26.4 3.3 %peer_rows.1 = (bf16[2,64,1024]{2,1,0:T(8,128)(2,1)S(1)}, f32[2,64,1024]{2,1,0:T(8,128)S(1)}, f32[32,128]{1,0:T(8,128)}) custom-call(bf16[128,512]{1,0:T(8,128)(2,1)S(1)} %collective-permute-done.peers.peer_x, bf16[2,512,1024]{2,1,0:T(8,128)(2,1)S(1)} %get-tuple-element.26.w_up, bf16[2,1024,512]{2,1,0:T(8,128)(2,1)S(1)} %get-tuple-element.27.w_down, ...), custom_call_target="tpu_custom_call" | custom-call | flops 268435456 | tf_op jit(solution)/shard_map/peer_rows/pallas_call | solution.py:386
  29.7 2.8 %all-to-all-start.1 = ((f32[32,1,128]{2,1,0:T(1,128)}), f32[32,1,128]{2,1,0:T(1,128)S(1)}, u32[]{:S(2)}, u32[]{:S(2)}) async-start(f32[32,1,128]{2,1,0:T(1,128)} %bitcast.5), calls=%async_computation.1 | async-start | bytes 32768 | tf_op jit(solution)/shard_map/all_to_all | solution.py:402
  32.5 0.0 collective-permute-done.1.peer_g
  32.5 12.6 %update.1 = (bf16[2,512,1024]{2,1,0:T(8,128)(2,1)}, bf16[2,1024,512]{2,1,0:T(8,128)(2,1)}, bf16[2,512,1024]{2,1,0:T(8,128)(2,1)}, bf16[2,512,1024]{2,1,0:T(8,128...) custom-call(bf16[128,1024]{1,0:T(8,128)(2,1)S(1)} %bitcast.12, ...), custom_call_target="tpu_custom_call" | custom-call | flops 1610612736 | bytes 25165824 | tf_op jit(solution)/shard_map/update/pallas_call | solution.py:411
  45.1 0.0 all-to-all-done.1
  45.1 1.6 %finish.1 = f32[16,128]{1,0:T(8,128)} custom-call(s32[1,128]{1,0:T(1,128)S(1)} %get-tuple-element.24.slot, f32[32,128]{1,0:T(8,128)S(1)} %bitcast.14, f32[16,128]{1,0:T(8,128)S(1)} %get-tuple-element.30.own, f32[1,128]{1,0:T(1,128)} %bitcast.20), custom_call_target="tpu_custom_call" | custom-call | tf_op jit(solution)/shard_map/finish/pallas_call | solution.py:448
  (1 shorter events, 0.0 us)
Async XLA Ops:
  19.4 7.0 %collective-permute-start = (bf16[128,512]{1,0:T(8,128)(2,1)S(1)}, bf16[128,512]{1,0:T(8,128)(2,1)S(1)}, u32[]{:S(2)}, u32[]{:S(2)}) collective-permute-start(bf16[128,512]{1,0:T(8,128)(2,1)S(1)} %get-tuple-element.42), channel_id=1, source_target_pairs={{0,16},{16,0},{1,17},{17,1},{2,18},{18,2},{3,19},{19,3},{4,20},{20... | collective-permute-start | bytes 393224 | tf_op jit(solution)/shard_map/ppermute | solution.py:359
  20.9 11.6 %collective-permute-start.1 = (bf16[128,512]{1,0:T(8,128)(2,1)S(1)}, bf16[128,512]{1,0:T(8,128)(2,1)S(1)}, u32[]{:S(2)}, u32[]{:S(2)}) collective-permute-start(bf16[128,512]{1,0:T(8,128)(2,1)S(1)} %get-tuple-element.41), channel_id=1, source_target_pairs={{0,16},{16,0},{1,17},{17,1},{2,18},{18,2},{3,19},{19,3},{4,20},{20... | collective-permute-start | bytes 393224 | tf_op jit(solution)/shard_map/ppermute | solution.py:359
  29.7 15.4 %all-to-all-start.1 = ((f32[32,1,128]{2,1,0:T(1,128)}), f32[32,1,128]{2,1,0:T(1,128)S(1)}, u32[]{:S(2)}, u32[]{:S(2)}) async-start(f32[32,1,128]{2,1,0:T(1,128)} %bitcast.5), calls=%async_computation.1 | async-start | bytes 32768 | tf_op jit(solution)/shard_map/all_to_all | solution.py:402

commit v3 on v2

v3 whole, which is shorter than its diff:
```python
import functools
import math

import jax
import jax.numpy as jnp
from jax import lax
from jax.experimental import pallas as pl
from jax.experimental.pallas import tpu as pltpu
from jax.sharding import PartitionSpec as P

CAP = 4

beta_first = 0.9
beta_second = 0.95
correct_first = 1.0 - 0.9**20
correct_second = 1.0 - 0.95**20
learn_rate = 0.002
adam_epsilon = 1e-08

BF = jnp.bfloat16
F32 = jnp.float32
EXACT = lax.Precision.HIGHEST
VMEM = pl.BlockSpec(memory_space=pltpu.VMEM)
SMEM = pl.BlockSpec(memory_space=pltpu.SMEM)
HBM = pl.BlockSpec(memory_space=pltpu.HBM)


def iota(shape, dim):
    return lax.broadcasted_iota(jnp.int32, shape, dim)


def dot(a, b, dims=((1,), (0,)), precision=None):
    return lax.dot_general(a, b, (dims, ((), ())), precision=precision, preferred_element_type=F32)


def gelu_parts(pre):
    normal_cdf = 0.5 * (1.0 + lax.erf(pre * 0.7071067811865476))
    density = jnp.exp(-0.5 * pre * pre) * 0.3989422804014327
    return (pre * normal_cdf, normal_cdf + pre * density)


def adam_step(weight, first, second, grad):
    new_first = beta_first * first.astype(F32) + (1.0 - beta_first) * grad
    new_second = beta_second * second.astype(F32) + ((1.0 - beta_second) * grad) * grad
    root = new_second * lax.rsqrt(new_second) + adam_epsilon * correct_second**0.5
    rate = learn_rate * correct_second**0.5 / correct_first
    update = (new_first * rate) * lax.rsqrt(root * root)
    moved = weight.astype(F32) - update
    return (moved.astype(BF), new_first.astype(BF), new_second.astype(BF))


def pack_kernel(labels, placement, tokens, cotangent, head, send, slot_out, own):
    experts = placement.shape[0]
    count, width = tokens.shape
    label = labels[...]
    regime = iota((experts, count), 0)
    held = jnp.zeros((experts, count), jnp.int32)
    for j in range(experts):
        held = jnp.where(regime == j, placement[j], held)
    chosen = held == label
    before = (iota((count, count), 0) < iota((count, count), 1)).astype(F32).astype(BF)
    earlier = dot(chosen.astype(F32).astype(BF), before)
    position = jnp.sum(jnp.where(chosen, earlier, 0.0), axis=0, keepdims=True).astype(jnp.int32)
    target = jnp.sum(jnp.where(chosen, regime, 0), axis=0, keepdims=True)
    slot = target * CAP + position
    slot_out[...] = slot
    pick = (iota((experts * CAP, count), 0) == slot).astype(F32).astype(BF)
    send[:, pl.ds(0, width)] = dot(pick, tokens[...]).astype(BF)
    send[:, pl.ds(width, width)] = dot(pick, cotangent[...]).astype(BF)
    own[...] = dot(head[...], tokens[...].astype(F32), ((1,), (1,)), EXACT)


def unmix(local_count, span):
    group = span // (local_count * CAP)
    row = iota((span, span), 0)
    source = row % group * (local_count * CAP) + row // group
    return (source == iota((span, span), 1)).astype(F32).astype(BF)


def forward_rows(expert, x, w_up, w_down, heads, local_count):
    group = x.shape[0] // CAP
    lanes = heads.shape[2]
    value, slant = gelu_parts(dot(x, w_up[expert]))
    value = value.astype(BF)
    out = dot(value, w_down[expert]).astype(BF)
    logit = dot(out, heads[0]) + dot(out, heads[1]) + dot(out, heads[2])
    place = iota((group, lanes), 1) // (lanes // (local_count * CAP))
    total = jnp.zeros((group, lanes), F32)
    for c in range(CAP):
        mine = place == expert * CAP + c
        total = jnp.where(mine, logit[c * group : (c + 1) * group], total)
    return value, slant, total


def own_kernel(
    recv, w_up, w_down, head, x_own, g_own, hidden, slope, part, heads, up_here, down_here, sems
):
    local_count, width, _ = w_up.shape
    copies = []
    for expert in range(local_count):
        for side, (there, here) in enumerate(((w_up, up_here), (w_down, down_here))):
            copy = pltpu.make_async_copy(there.at[expert], here.at[expert], sems.at[expert, side])
            copy.start()
            copies.append(copy)
    span = recv.shape[0]
    rows = span // local_count
    both = dot(unmix(local_count, span), recv[...]).astype(BF)
    for expert in range(local_count):
        x_own[expert] = both[expert * rows : (expert + 1) * rows, :width]
        g_own[expert] = both[expert * rows : (expert + 1) * rows, width:]
    tiled = jnp.concatenate([head[...]] * (local_count * CAP), axis=0).T
    for i in range(3):
        piece = tiled.astype(BF)
        heads[i] = piece
        tiled = tiled - piece.astype(F32)
    total = None
    for expert in range(local_count):
        copies[2 * expert].wait()
        copies[2 * expert + 1].wait()
        value, slant, logit = forward_rows(
            expert, x_own[expert], up_here, down_here, heads, local_count
        )
        hidden[expert] = value
        slope[expert] = slant
        total = logit if total is None else total + logit
    part[...] = total


def peer_kernel(copies, peers, w_up, w_down, heads, part, x_peer, hidden, slope, out):
    local_count = w_up.shape[0]
    span = peers.shape[0] // (copies - 1)
    rows = span // local_count
    group = rows // CAP
    here = lax.axis_index("dp")
    select = unmix(local_count, span)
    out[pl.ds(pl.multiple_of(here * group, 8), group), :] = part[...]
    for step in range(1, copies):
        at = pl.ds((step - 1) * rows, rows)
        x = dot(select, peers[pl.ds((step - 1) * span, span), :]).astype(BF)
        total = None
        for expert in range(local_count):
            mine = x[expert * rows : (expert + 1) * rows]
            x_peer[expert, at, :] = mine
            value, slant, logit = forward_rows(expert, mine, w_up, w_down, heads, local_count)
            hidden[expert, at, :] = value
            slope[expert, at, :] = slant
            total = logit if total is None else total + logit
        owner = lax.rem(here - step + copies, copies)
        out[pl.ds(pl.multiple_of(owner * group, 8), group), :] = total


def update_kernel(
    copies,
    x_own,
    x_peer,
    g_own,
    peer_g,
    hidden_own,
    hidden_peer,
    slope_own,
    slope_peer,
    w_up,
    w_down,
    up_m,
    up_v,
    down_m,
    down_v,
    up_next,
    down_next,
    up_m_next,
    up_v_next,
    down_m_next,
    down_v_next,
    ups,
    downs,
    x_t,
    g_all,
    hidden_grad,
    up_grad,
    down_grad,
    sems,
):
    local_count, width, hidden_count = w_up.shape
    up_tile = up_grad.shape[1]
    down_tile = down_grad.shape[1]
    blocks = []
    for expert in range(local_count):
        blocks += [(expert, True, step) for step in range(hidden_count // down_tile)]
        blocks += [(expert, False, step) for step in range(width // up_tile)]

    def moves(number, out):
        expert, down, step = blocks[number]
        tile, held = (down_tile, downs) if down else (up_tile, ups)
        pairs = (
            ((w_down, down_next), (down_m, down_m_next), (down_v, down_v_next))
            if down
            else ((w_up, up_next), (up_m, up_m_next), (up_v, up_v_next))
        )
        here = pl.ds(step * tile, tile)
        return [
            pltpu.make_async_copy(
                held.at[i, expert, here] if out else pair[0].at[expert, here],
                pair[1].at[expert, here] if out else held.at[i, expert, here],
                sems.at[int(out), number, i],
            )
            for i, pair in enumerate(pairs)
        ]

    for number in range(len(blocks)):
        for move in moves(number, False):
            move.start()

    span = peer_g.shape[0] // (copies - 1)
    rows = span // local_count
    select = unmix(local_count, span)
    for step in range(1, copies):
        g = dot(select, peer_g[pl.ds((step - 1) * span, span), :]).astype(BF)
        for expert in range(local_count):
            g_all[expert, pl.ds(step * rows, rows), :] = g[expert * rows : (expert + 1) * rows]
    for expert in range(local_count):
        g_all[expert, pl.ds(0, rows), :] = g_own[expert]
        x_t[expert] = jnp.concatenate([x_own[expert], x_peer[expert]], axis=0).T

    def stage(number):
        expert, down, step = blocks[number]
        if down:
            here = pl.ds(step * down_tile, down_tile)
            back = dot(g_all[expert], downs[0, expert, here], ((1,), (1,)))
            slope = jnp.concatenate([slope_own[expert, :, here], slope_peer[expert, :, here]], axis=0)
            hidden_grad[expert, :, here] = (back * slope).astype(BF)
            hidden = jnp.concatenate([hidden_own[expert, :, here], hidden_peer[expert, :, here]], axis=0)
            down_grad[number % 2] = dot(hidden.T, g_all[expert])
        else:
            here = pl.ds(step * up_tile, up_tile)
            up_grad[number % 2] = dot(x_t[expert, here, :], hidden_grad[expert])

    def settle(number):
        expert, down, step = blocks[number]
        held, grads = (downs, down_grad) if down else (ups, up_grad)
        count = grads.shape[1]
        tile = math.gcd(count, 32 if down else 16)
        for start in range(0, count, tile):
            at = pl.ds(step * count + start, tile)
            new = adam_step(
                *[held[i, expert, at] for i in range(3)], grads[number % 2, pl.ds(start, tile)]
            )
            for i in range(3):
                held[i, expert, at] = new[i]

    for move in moves(0, False):
        move.wait()
    stage(0)
    for number in range(len(blocks)):
        if number + 1 < len(blocks):
            for move in moves(number + 1, False):
                move.wait()
            stage(number + 1)
        settle(number)
        for move in moves(number, True):
            move.start()
    for number in range(len(blocks)):
        for move in moves(number, True):
            move.wait()


def finish_kernel(holders, slot, returned, own, mass, out):
    pixels, count = own.shape
    lanes = returned.shape[1]
    copies = returned.shape[0] // holders
    total = returned[pl.ds(0, holders), :]
    for part in range(1, copies):
        total = total + returned[pl.ds(part * holders, holders), :]
    places = lanes // pixels
    holder = slot[...] // places
    place = slot[...] % places
    pick = (iota((holders, count), 0) == holder).astype(F32)
    spread = dot(total, pick, ((0,), (0,)), EXACT)
    logits = own[...]
    for q in range(places):
        logits = logits + jnp.where(place == q, spread[q * pixels : (q + 1) * pixels, :], 0.0)
    positive = jax.nn.softplus(logits) + 0.1
    out[...] = mass[...] * positive / jnp.sum(positive, axis=0, keepdims=True)


def shape(*args):
    return jax.ShapeDtypeStruct(*args)


def stay(value):
    return pltpu.with_memory_space_constraint(value, pltpu.HBM)


def limit(mib):
    return pltpu.CompilerParams(vmem_limit_bytes=mib << 20)


def local(
    tokens,
    cotangent,
    labels,
    placement,
    mass,
    w_head,
    w_up,
    w_down,
    up_moment,
    up_square,
    down_moment,
    down_square,
):
    w_up, w_down, up_moment, up_square, down_moment, down_square = [
        stay(value) for value in (w_up, w_down, up_moment, up_square, down_moment, down_square)
    ]
    experts = placement.shape[0]
    count, width = tokens.shape
    pixels = w_head.shape[1]
    local_count, _, hidden_count = w_up.shape
    holders = lax.axis_size("expert")
    copies = lax.axis_size("dp")
    sources = holders * copies
    lanes = local_count * CAP * pixels
    rows = holders * CAP
    head = w_head.T
    up_shape = shape(w_up.shape, BF)
    down_shape = shape(w_down.shape, BF)
    one_product = 2 * rows * width * hidden_count * local_count

    send, slot, own = pl.pallas_call(
        pack_kernel,
        out_shape=(
            shape((experts * CAP, 2 * width), BF),
            shape((1, count), jnp.int32),
            shape((pixels, count), F32),
        ),
        in_specs=[VMEM, SMEM, VMEM, VMEM, VMEM],
        out_specs=(VMEM, VMEM, VMEM),
        compiler_params=limit(4),
        name="pack",
    )(stay(labels.reshape(1, count)), stay(placement), stay(tokens), stay(cotangent), stay(head))

    recv = lax.all_to_all(send, "expert", split_axis=0, concat_axis=0, tiled=True)

    def to_peers(value):
        moved = [
            lax.ppermute(value, "dp", [(i, (i + step) % copies) for i in range(copies)])
            for step in range(1, copies)
        ]
        return moved[0] if copies == 2 else jnp.concatenate(moved, axis=0)

    peer_x = to_peers(recv[:, :width])
    peer_g = to_peers(recv[:, width:])

    x_own, g_own, hidden_own, slope_own, part, heads, up_here, down_here = pl.pallas_call(
        own_kernel,
        out_shape=(
            shape((local_count, rows, width), BF),
            shape((local_count, rows, width), BF),
            shape((local_count, rows, hidden_count), BF),
            shape((local_count, rows, hidden_count), F32),
            shape((holders, lanes), F32),
            pltpu.VMEM((3, width, lanes), BF),
            pltpu.VMEM(w_up.shape, BF),
            pltpu.VMEM(w_down.shape, BF),
        ),
        in_specs=[VMEM, HBM, HBM, VMEM],
        out_specs=(VMEM,) * 8,
        scratch_shapes=[pltpu.SemaphoreType.DMA((local_count, 2))],
        compiler_params=limit(16),
        cost_estimate=pl.CostEstimate(
            flops=4 * one_product,
            bytes_accessed=4 * width * hidden_count * local_count,
            transcendentals=0,
        ),
        name="own_rows",
    )(recv, w_up, w_down, stay(head))

    others = rows * (copies - 1)
    x_peer, hidden_peer, slope_peer, scores = pl.pallas_call(
        functools.partial(peer_kernel, copies),
        out_shape=(
            shape((local_count, others, width), BF),
            shape((local_count, others, hidden_count), BF),
            shape((local_count, others, hidden_count), F32),
            shape((sources, lanes), F32),
        ),
        in_specs=[VMEM] * 5,
        out_specs=(VMEM,) * 4,
        compiler_params=limit(16),
        cost_estimate=pl.CostEstimate(flops=2 * one_product, bytes_accessed=0, transcendentals=0),
        name="peer_rows",
    )(peer_x, up_here, down_here, heads, part)

    returned = lax.all_to_all(
        scores.reshape(sources, 1, lanes),
        ("dp", "expert"),
        split_axis=0,
        concat_axis=0,
        tiled=True,
    ).reshape(sources, lanes)

    up_tile = math.gcd(width, 128)
    down_tile = math.gcd(hidden_count, 256)
    blocks = local_count * (width // up_tile + hidden_count // down_tile)
    updates = pl.pallas_call(
        functools.partial(update_kernel, copies),
        out_shape=(up_shape, down_shape, up_shape, up_shape, down_shape, down_shape),
        in_specs=[VMEM] * 8 + [HBM] * 6,
        out_specs=(HBM,) * 6,
        scratch_shapes=[
            pltpu.VMEM((3,) + w_up.shape, BF),
            pltpu.VMEM((3,) + w_down.shape, BF),
            pltpu.VMEM((local_count, width, rows * copies), BF),
            pltpu.VMEM((local_count, rows * copies, width), BF),
            pltpu.VMEM((local_count, rows * copies, hidden_count), BF),
            pltpu.VMEM((2, up_tile, hidden_count), F32),
            pltpu.VMEM((2, down_tile, width), F32),
            pltpu.SemaphoreType.DMA((2, blocks, 3)),
        ],
        compiler_params=limit(28),
        cost_estimate=pl.CostEstimate(
            flops=6 * one_product * copies,
            bytes_accessed=24 * width * hidden_count * local_count,
            transcendentals=0,
        ),
        name="update",
    )(
        x_own,
        x_peer,
        g_own,
        peer_g,
        hidden_own,
        hidden_peer,
        slope_own,
        slope_peer,
        w_up,
        w_down,
        up_moment,
        up_square,
        down_moment,
        down_square,
    )

    fine = pl.pallas_call(
        functools.partial(finish_kernel, holders),
        out_shape=shape((pixels, count), F32),
        in_specs=[VMEM] * 4,
        out_specs=VMEM,
        compiler_params=limit(2),
        name="finish",
    )(slot, returned, own, mass.reshape(1, count))
    return (fine.T,) + tuple(updates)


def solution(mesh):
    tokens = P(("dp", "expert"), None)
    up = P("expert", None, "dp")
    down = P("expert", "dp", None)
    return jax.shard_map(
        local,
        mesh=mesh,
        in_specs=(tokens, tokens, tokens, P(), P(("dp", "expert")), P())
        + (up, down, up, up, down, down),
        out_specs=(tokens, up, down, up, up, down, down),
        check_vma=False,
    )
```

time: 47 us -> 43.2 us (0.919)
  Pallas kernels: 23.9 us -> 19.5 us
  waiting for transfers between devices: 0.01 us -> 0.63 us
    pallas_call x1, Pallas kernels: 3.29 us -> 1.95 us  [local(): pl.pallas_call(functools.partial(peer_kernel, copies), out_shape=(shape((...]
    pallas_call x1, Pallas kernels: 4.93 us -> 3.71 us  [local(): pl.pallas_call(own_kernel, out_shape=(shape((local_count, rows, width), B...]
    pallas_call x1, Pallas kernels: 12.6 us -> 11.4 us  [local(): pl.pallas_call(functools.partial(update_kernel, copies), out_shape=(up_sh...]
    pallas_call x1, Pallas kernels: 1.55 us -> 0.9 us  [local(): pl.pallas_call(functools.partial(finish_kernel, holders), out_shape=shape...]
    ppermute x2, waiting for transfers between devices: 0.01 us -> 0.63 us  [to_peers(): lax.ppermute(value, 'dp', [(i, (i + step) % copies) for i in range(copies)])]
  transfers between devices with their start and end apart: 3 -> 3, of which waited for: 0 -> 1; matrix products, arithmetic and copies ran while one was open for 0% -> 0% of each run, Pallas kernels for 45% -> 40%
where the time goes in v3:
time: 43.2 us; the launch traced here: 42.9 us
  Pallas kernels  19.5 us (45%)
  blocking collectives  17.2 us (40%)
  starting transfers between devices  4.88 us (11%)
  between operations  0.7 us (2%)
  waiting for transfers between devices  0.63 us (1%)
    all_to_all x1, blocking collectives, local(): lax.all_to_all(send, 'expert', split_axis=0, concat_axis=0, tiled=True)  17.2 us
    pallas_call x1, Pallas kernels, local(): pl.pallas_call(functools.partial(update_kernel, copies), out_shape=(up_sh...  11.4 us
    pallas_call x1, Pallas kernels, local(): pl.pallas_call(own_kernel, out_shape=(shape((local_count, rows, width), B...  3.71 us
    all_to_all x1, starting transfers between devices, local(): lax.all_to_all(scores.reshape(sources, 1, lanes), ('dp', 'expert'), split...  2.79 us
    ppermute x2, starting transfers between devices, to_peers(): lax.ppermute(value, 'dp', [(i, (i + step) % copies) for i in range(copies)])  2.09 us
    pallas_call x1, Pallas kernels, local(): pl.pallas_call(functools.partial(peer_kernel, copies), out_shape=(shape((...  1.95 us
    pallas_call x1, Pallas kernels, local(): pl.pallas_call(pack_kernel, out_shape=(shape((experts * CAP, 2 * width),...  1.5 us
    pallas_call x1, Pallas kernels, local(): pl.pallas_call(functools.partial(finish_kernel, holders), out_shape=shape...  0.9 us
  transfers between devices with their start and end apart: 3, of which 1 were waited for; matrix products, arithmetic and copies ran while one was open for 0% of the time, Pallas kernels for 40%

profile of v3, /device:TPU:0, one launch (start us, length us, event | category | flops | bytes accessed | tf_op | source)
XLA Modules:
  0.0 42.9 jit_solution(14914319560835257929)
XLA Ops:
  0.6 1.5 %pack.1 = (bf16[128,1024]{1,0:T(8,128)(2,1)S(1)}, s32[1,128]{1,0:T(1,128)S(1)}, f32[16,128]{1,0:T(8,128)S(1)}) custom-call(s32[1,128]{1,0:T(1,128)} %bitcast.18, s32[32]{0:T(128)} %placement.1, bf16[128,512]{1,0:T(8,128)(2,1)} %tokens.1, bf16[128,512]{1,0:T(8,128)(2,1)} %cotangent.1, f32[16,512]{1,0:T(8,128)} %bitcast.15), custom_call_target="tpu_custom_call" | custom-call | tf_op jit(solution)/shard_map/pack/pallas_call | solution.py:328
  2.1 17.2 %all_to_all.16 = bf16[16,8,1024]{2,1,0:T(8,128)(2,1)S(1)} all-to-all(bf16[16,8,1024]{2,1,0:T(8,128)(2,1)S(1)} %bitcast.12), channel_id=1, replica_groups=mesh['dp'=2,'expert'=16] {'expert'}, dimensions={0} | all-to-all | bytes 524288 | tf_op jit(solution)/shard_map/all_to_all | solution.py:341
  19.4 1.6 %collective-permute-start = (bf16[128,512]{1,0:T(8,128)(2,1)S(1)}, bf16[128,512]{1,0:T(8,128)(2,1)S(1)}, u32[]{:S(2)}, u32[]{:S(2)}) collective-permute-start(bf16[128,512]{1,0:T(8,128)(2,1)S(1)} %get-tuple-element.50), channel_id=1, source_target_pairs={{0,16},{16,0},{1,17},{17,1},{2,18},{18,2},{3,19},{19,3},{4,20},{20... | collective-permute-start | bytes 393224 | tf_op jit(solution)/shard_map/ppermute | solution.py:345
  20.9 0.5 %collective-permute-start.1 = (bf16[128,512]{1,0:T(8,128)(2,1)S(1)}, bf16[128,512]{1,0:T(8,128)(2,1)S(1)}, u32[]{:S(2)}, u32[]{:S(2)}) collective-permute-start(bf16[128,512]{1,0:T(8,128)(2,1)S(1)} %get-tuple-element.49), channel_id=1, source_target_pairs={{0,16},{16,0},{1,17},{17,1},{2,18},{18,2},{3,19},{19,3},{4,20},{20... | collective-permute-start | bytes 393224 | tf_op jit(solution)/shard_map/ppermute | solution.py:345
  21.5 3.7 %own_rows.1 = (bf16[2,64,512]{2,1,0:T(8,128)(2,1)S(1)}, bf16[2,64,512]{2,1,0:T(8,128)(2,1)S(1)}, bf16[2,64,1024]{2,1,0:T(8,128)(2,1)S(1)}, f32[2,64,1024]{2,1,0:...) custom-call(bf16[128,1024]{1,0:T(8,128)(2,1)S(1)} %bitcast.11, ...), custom_call_target="tpu_custom_call" | custom-call | flops 536870912 | bytes 4194304 | tf_op jit(solution)/shard_map/own_rows/pallas_call | solution.py:353
  25.2 0.6 %collective-permute-done.peers = bf16[128,512]{1,0:T(8,128)(2,1)S(1)} collective-permute-done((bf16[128,512]{1,0:T(8,128)(2,1)S(1)}, bf16[128,512]{1,0:T(8,128)(2,1)S(1)}, u32[]{:S(2)}, u32[]{:S(2)}) %collective-permute-start) | collective-permute-done | bytes 131104 | tf_op jit(solution)/shard_map/ppermute | solution.py:345
  25.8 2.0 %peer_rows.1 = (bf16[2,64,512]{2,1,0:T(8,128)(2,1)S(1)}, bf16[2,64,1024]{2,1,0:T(8,128)(2,1)S(1)}, f32[2,64,1024]{2,1,0:T(8,128)S(1)}, f32[32,128]{1,0:T(8,128)}) custom-call(bf16[128,512]{1,0:T(8,128)(2,1)S(1)} %collective-permute-done.peers, bf16[2,512,1024]{2,1,0:T(8,128)(2,1)S(1)} %get-tuple-element.30.w_up, ...), custom_call_target="tpu_custom_call" | custom-call | flops 268435456 | tf_op jit(solution)/shard_map/peer_rows/pallas_call | solution.py:378
  27.8 2.8 %all-to-all-start.1 = ((f32[32,1,128]{2,1,0:T(1,128)}), f32[32,1,128]{2,1,0:T(1,128)S(1)}, u32[]{:S(2)}, u32[]{:S(2)}) async-start(f32[32,1,128]{2,1,0:T(1,128)} %bitcast.5), calls=%async_computation.1 | async-start | bytes 32768 | tf_op jit(solution)/shard_map/all_to_all | solution.py:393
  30.6 0.0 collective-permute-done.1.peer_g
  30.6 0.0 copy-start
  30.6 11.4 %update.1 = (bf16[2,512,1024]{2,1,0:T(8,128)(2,1)}, bf16[2,1024,512]{2,1,0:T(8,128)(2,1)}, bf16[2,512,1024]{2,1,0:T(8,128)(2,1)}, bf16[2,512,1024]{2,1,0:T(8,128...) custom-call(bf16[2,64,512]{2,1,0:T(8,128)(2,1)S(1)} %get-tuple-element.36.x_own, ...), custom_call_target="tpu_custom_call" | custom-call | flops 1610612736 | bytes 25165824 | tf_op jit(solution)/shard_map/update/pallas_call | solution.py:404
  42.0 0.0 all-to-all-done.1
  42.0 0.0 copy-done
  42.0 0.9 %finish.1 = f32[16,128]{1,0:T(8,128)} custom-call(s32[1,128]{1,0:T(1,128)S(1)} %get-tuple-element.28.slot, f32[32,128]{1,0:T(8,128)S(1)} %bitcast.13, f32[16,128]{1,0:T(8,128)S(1)} %get-tuple-element.35.own, f32[1,128]{1,0:T(1,128)S(1)} %bitcast.14), custom_call_target="tpu_custom_call" | custom-call | tf_op jit(solution)/shard_map/finish/pallas_call | solution.py:443
  (1 shorter events, 0.0 us)
Async XLA Ops:
  19.4 6.4 %collective-permute-start = (bf16[128,512]{1,0:T(8,128)(2,1)S(1)}, bf16[128,512]{1,0:T(8,128)(2,1)S(1)}, u32[]{:S(2)}, u32[]{:S(2)}) collective-permute-start(bf16[128,512]{1,0:T(8,128)(2,1)S(1)} %get-tuple-element.50), channel_id=1, source_target_pairs={{0,16},{16,0},{1,17},{17,1},{2,18},{18,2},{3,19},{19,3},{4,20},{20... | collective-permute-start | bytes 393224 | tf_op jit(solution)/shard_map/ppermute | solution.py:345
  20.9 9.6 %collective-permute-start.1 = (bf16[128,512]{1,0:T(8,128)(2,1)S(1)}, bf16[128,512]{1,0:T(8,128)(2,1)S(1)}, u32[]{:S(2)}, u32[]{:S(2)}) collective-permute-start(bf16[128,512]{1,0:T(8,128)(2,1)S(1)} %get-tuple-element.49), channel_id=1, source_target_pairs={{0,16},{16,0},{1,17},{17,1},{2,18},{18,2},{3,19},{19,3},{4,20},{20... | collective-permute-start | bytes 393224 | tf_op jit(solution)/shard_map/ppermute | solution.py:345
  27.8 14.2 %all-to-all-start.1 = ((f32[32,1,128]{2,1,0:T(1,128)}), f32[32,1,128]{2,1,0:T(1,128)S(1)}, u32[]{:S(2)}, u32[]{:S(2)}) async-start(f32[32,1,128]{2,1,0:T(1,128)} %bitcast.5), calls=%async_computation.1 | async-start | bytes 32768 | tf_op jit(solution)/shard_map/all_to_all | solution.py:393
  30.6 11.4 %copy-start = (f32[128]{0:T(128)S(1)}, f32[128]{0:T(128)}, u32[]{:S(2)}) copy-start(f32[128]{0:T(128)} %param.16) | copy-start | bytes 1540

commit v4 on v3

--- a/solution.py
+++ b/solution.py
@@ -9,6 +9,7 @@
 from jax.sharding import PartitionSpec as P
 
 CAP = 4
+AHEAD = 2.0
 
 beta_first = 0.9
 beta_second = 0.95
@@ -49,7 +50,7 @@
     return (moved.astype(BF), new_first.astype(BF), new_second.astype(BF))
 
 
-def pack_kernel(labels, placement, tokens, cotangent, head, send, slot_out, own):
+def pack_kernel(labels, placement, tokens, cotangent, send, slot_out):
     experts = placement.shape[0]
     count, width = tokens.shape
     label = labels[...]
@@ -67,7 +68,6 @@
     pick = (iota((experts * CAP, count), 0) == slot).astype(F32).astype(BF)
     send[:, pl.ds(0, width)] = dot(pick, tokens[...]).astype(BF)
     send[:, pl.ds(width, width)] = dot(pick, cotangent[...]).astype(BF)
-    own[...] = dot(head[...], tokens[...].astype(F32), ((1,), (1,)), EXACT)
 
 
 def unmix(local_count, span):
@@ -77,29 +77,56 @@
     return (source == iota((span, span), 1)).astype(F32).astype(BF)
 
 
-def forward_rows(expert, x, w_up, w_down, heads, local_count):
-    group = x.shape[0] // CAP
+def score_rows(expert, value, w_down, heads, local_count):
+    group = value.shape[0] // CAP
     lanes = heads.shape[2]
-    value, slant = gelu_parts(dot(x, w_up[expert]))
-    value = value.astype(BF)
-    out = dot(value, w_down[expert]).astype(BF)
+    out = dot(value, w_down).astype(BF)
     logit = dot(out, heads[0]) + dot(out, heads[1]) + dot(out, heads[2])
     place = iota((group, lanes), 1) // (lanes // (local_count * CAP))
     total = jnp.zeros((group, lanes), F32)
     for c in range(CAP):
         mine = place == expert * CAP + c
         total = jnp.where(mine, logit[c * group : (c + 1) * group], total)
-    return value, slant, total
+    return total
 
 
 def own_kernel(
-    recv, w_up, w_down, head, x_own, g_own, hidden, slope, part, heads, up_here, down_here, sems
+    recv,
+    w_up,
+    w_down,
+    head,
+    tokens,
+    x_own,
+    g_own,
+    hidden,
+    slope,
+    part,
+    heads,
+    own,
+    up_here,
+    down_first,
+    down_rest,
+    head_here,
+    tokens_here,
+    sems,
+    small_sems,
 ):
     local_count, width, _ = w_up.shape
+    small = [
+        pltpu.make_async_copy(head, head_here, small_sems.at[0]),
+        pltpu.make_async_copy(tokens, tokens_here, small_sems.at[1]),
+    ]
+    for copy in small:
+        copy.start()
     copies = []
-    for expert in range(local_count):
-        for side, (there, here) in enumerate(((w_up, up_here), (w_down, down_here))):
-            copy = pltpu.make_async_copy(there.at[expert], here.at[expert], sems.at[expert, side])
+    for side in range(2):
+        for expert in range(local_count):
+            if side == 0:
+                there, here = w_up.at[expert], up_here.at[expert]
+            else:
+                there = w_down.at[expert]
+                here = down_rest.at[expert - 1] if expert else down_first
+            copy = pltpu.make_async_copy(there, here, sems.at[expert, side])
             copy.start()
             copies.append(copy)
     span = recv.shape[0]
@@ -108,25 +135,31 @@
     for expert in range(local_count):
         x_own[expert] = both[expert * rows : (expert + 1) * rows, :width]
         g_own[expert] = both[expert * rows : (expert + 1) * rows, width:]
-    tiled = jnp.concatenate([head[...]] * (local_count * CAP), axis=0).T
+    for copy in small:
+        copy.wait()
+    rest = jnp.concatenate([head_here[...]] * (local_count * CAP), axis=0).T
     for i in range(3):
-        piece = tiled.astype(BF)
+        piece = rest.astype(BF)
         heads[i] = piece
-        tiled = tiled - piece.astype(F32)
+        rest = rest - piece.astype(F32)
+    own[...] = dot(head_here[...], tokens_here[...].astype(F32), ((1,), (1,)), EXACT)
+    for expert in range(local_count):
+        copies[expert].wait()
+        value, slant = gelu_parts(dot(x_own[expert], up_here[expert]))
+        hidden[expert] = value.astype(BF)
+        slope[expert] = slant
     total = None
     for expert in range(local_count):
-        copies[2 * expert].wait()
-        copies[2 * expert + 1].wait()
-        value, slant, logit = forward_rows(
-            expert, x_own[expert], up_here, down_here, heads, local_count
-        )
-        hidden[expert] = value
-        slope[expert] = slant
+        copies[local_count + expert].wait()
+        weight = down_rest[expert - 1] if expert else down_first[...]
+        logit = score_rows(expert, hidden[expert], weight, heads, local_count)
         total = logit if total is None else total + logit
     part[...] = total
 
 
-def peer_kernel(copies, peers, w_up, w_down, heads, part, x_peer, hidden, slope, out):
+def peer_kernel(
+    copies, peers, w_up, down_first, down_rest, heads, part, x_peer, hidden, slope, out
+):
     local_count = w_up.shape[0]
     span = peers.shape[0] // (copies - 1)
     rows = span // local_count
@@ -141,12 +174,37 @@
         for expert in range(local_count):
             mine = x[expert * rows : (expert + 1) * rows]
             x_peer[expert, at, :] = mine
-            value, slant, logit = forward_rows(expert, mine, w_up, w_down, heads, local_count)
+            value, slant = gelu_parts(dot(mine, w_up[expert]))
+            value = value.astype(BF)
             hidden[expert, at, :] = value
+            weight = down_rest[expert - 1] if expert else down_first[...]
+            logit = score_rows(expert, value, weight, heads, local_count)
             slope[expert, at, :] = slant
             total = logit if total is None else total + logit
         owner = lax.rem(here - step + copies, copies)
         out[pl.ds(pl.multiple_of(owner * group, 8), group), :] = total
+
+
+def graded(total, small_first, small_last):
+    if total % 128:
+        return [total]
+    sizes = [total // 8, total // 8, total // 4, total // 2] if small_first else [total // 2] * 2
+    if small_last:
+        sizes = [total // 2, total // 4, total // 8, total // 8]
+    return sizes
+
+
+def update_blocks(local_count, width, hidden_count):
+    blocks = []
+    for expert in range(local_count):
+        for down in (True, False):
+            start = 0
+            first = expert == 0 and down
+            last = expert == local_count - 1 and not down
+            for size in graded(hidden_count if down else width, first, last):
+                blocks.append((expert, down, start, size))
+                start += size
+    return blocks
 
 
 def update_kernel(
@@ -181,22 +239,20 @@
     sems,
 ):
     local_count, width, hidden_count = w_up.shape
-    up_tile = up_grad.shape[1]
-    down_tile = down_grad.shape[1]
-    blocks = []
-    for expert in range(local_count):
-        blocks += [(expert, True, step) for step in range(hidden_count // down_tile)]
-        blocks += [(expert, False, step) for step in range(width // up_tile)]
+    blocks = update_blocks(local_count, width, hidden_count)
+
+    def block_rows(block):
+        return block[3] * (width if block[1] else hidden_count) / (width * hidden_count)
 
     def moves(number, out):
-        expert, down, step = blocks[number]
-        tile, held = (down_tile, downs) if down else (up_tile, ups)
+        expert, down, start, size = blocks[number]
+        held = downs if down else ups
         pairs = (
             ((w_down, down_next), (down_m, down_m_next), (down_v, down_v_next))
             if down
             else ((w_up, up_next), (up_m, up_m_next), (up_v, up_v_next))
         )
-        here = pl.ds(step * tile, tile)
+        here = pl.ds(start, size)
         return [
             pltpu.make_async_copy(
                 held.at[i, expert, here] if out else pair[0].at[expert, here],
@@ -206,8 +262,19 @@
             for i, pair in enumerate(pairs)
         ]
 
-    for number in range(len(blocks)):
-        for move in moves(number, False):
+    due = []
+    asked = 0
+    for number in range(len(blocks) + 1):
+        due.append([])
+        done = sum(block_rows(block) for block in blocks[:number])
+        while asked < len(blocks) and (
+            asked <= number or sum(block_rows(block) for block in blocks[: asked + 1]) - done <= AHEAD
+        ):
+            due[number].append(asked)
+            asked += 1
+
+    for other in due[0]:
+        for move in moves(other, False):
             move.start()
 
     span = peer_g.shape[0] // (copies - 1)
@@ -222,27 +289,26 @@
         x_t[expert] = jnp.concatenate([x_own[expert], x_peer[expert]], axis=0).T
 
     def stage(number):
-        expert, down, step = blocks[number]
+        expert, down, start, size = blocks[number]
         if down:
-            here = pl.ds(step * down_tile, down_tile)
+            here = pl.ds(start, size)
             back = dot(g_all[expert], downs[0, expert, here], ((1,), (1,)))
             slope = jnp.concatenate([slope_own[expert, :, here], slope_peer[expert, :, here]], axis=0)
             hidden_grad[expert, :, here] = (back * slope).astype(BF)
             hidden = jnp.concatenate([hidden_own[expert, :, here], hidden_peer[expert, :, here]], axis=0)
-            down_grad[number % 2] = dot(hidden.T, g_all[expert])
+            down_grad[number % 2, pl.ds(0, size)] = dot(hidden.T, g_all[expert])
         else:
-            here = pl.ds(step * up_tile, up_tile)
-            up_grad[number % 2] = dot(x_t[expert, here, :], hidden_grad[expert])
+            here = pl.ds(start, size)
+            up_grad[number % 2, pl.ds(0, size)] = dot(x_t[expert, here, :], hidden_grad[expert])
 
     def settle(number):
-        expert, down, step = blocks[number]
+        expert, down, start, size = blocks[number]
         held, grads = (downs, down_grad) if down else (ups, up_grad)
-        count = grads.shape[1]
-        tile = math.gcd(count, 32 if down else 16)
-        for start in range(0, count, tile):
-            at = pl.ds(step * count + start, tile)
+        tile = math.gcd(size, 32 if down else 16)
+        for row in range(0, size, tile):
+            at = pl.ds(start + row, tile)
             new = adam_step(
-                *[held[i, expert, at] for i in range(3)], grads[number % 2, pl.ds(start, tile)]
+                *[held[i, expert, at] for i in range(3)], grads[number % 2, pl.ds(row, tile)]
             )
             for i in range(3):
                 held[i, expert, at] = new[i]
@@ -251,6 +317,9 @@
         move.wait()
     stage(0)
     for number in range(len(blocks)):
+        for other in due[number + 1]:
+            for move in moves(other, False):
+                move.start()
         if number + 1 < len(blocks):
             for move in moves(number + 1, False):
                 move.wait()
@@ -325,18 +394,17 @@
     down_shape = shape(w_down.shape, BF)
     one_product = 2 * rows * width * hidden_count * local_count
 
-    send, slot, own = pl.pallas_call(
+    send, slot = pl.pallas_call(
         pack_kernel,
         out_shape=(
             shape((experts * CAP, 2 * width), BF),
             shape((1, count), jnp.int32),
-            shape((pixels, count), F32),
         ),
-        in_specs=[VMEM, SMEM, VMEM, VMEM, VMEM],
-        out_specs=(VMEM, VMEM, VMEM),
+        in_specs=[VMEM, SMEM, VMEM, VMEM],
+        out_specs=(VMEM, VMEM),
         compiler_params=limit(4),
         name="pack",
-    )(stay(labels.reshape(1, count)), stay(placement), stay(tokens), stay(cotangent), stay(head))
+    )(stay(labels.reshape(1, count)), stay(placement), stay(tokens), stay(cotangent))
 
     recv = lax.all_to_all(send, "expert", split_axis=0, concat_axis=0, tiled=True)
 
@@ -348,9 +416,10 @@
         return moved[0] if copies == 2 else jnp.concatenate(moved, axis=0)
 
     peer_x = to_peers(recv[:, :width])
-    peer_g = to_peers(recv[:, width:])
-
-    x_own, g_own, hidden_own, slope_own, part, heads, up_here, down_here = pl.pallas_call(
+
+    (
+        x_own, g_own, hidden_own, slope_own, part, heads, own, up_here, down_first, down_rest
+    ) = pl.pallas_call(
         own_kernel,
         out_shape=(
             shape((local_count, rows, width), BF),
@@ -359,12 +428,19 @@
             shape((local_count, rows, hidden_count), F32),
             shape((holders, lanes), F32),
             pltpu.VMEM((3, width, lanes), BF),
+            shape((pixels, count), F32),
             pltpu.VMEM(w_up.shape, BF),
-            pltpu.VMEM(w_down.shape, BF),
+            pltpu.VMEM(w_down.shape[1:], BF),
+            pltpu.VMEM((local_count - 1,) + w_down.shape[1:], BF),
         ),
-        in_specs=[VMEM, HBM, HBM, VMEM],
-        out_specs=(VMEM,) * 8,
-        scratch_shapes=[pltpu.SemaphoreType.DMA((local_count, 2))],
+        in_specs=[VMEM, HBM, HBM, HBM, HBM],
+        out_specs=(VMEM,) * 10,
+        scratch_shapes=[
+            pltpu.VMEM(head.shape, F32),
+            pltpu.VMEM(tokens.shape, BF),
+            pltpu.SemaphoreType.DMA((local_count, 2)),
+            pltpu.SemaphoreType.DMA((2,)),
+        ],
         compiler_params=limit(16),
         cost_estimate=pl.CostEstimate(
             flops=4 * one_product,
@@ -372,8 +448,10 @@
             transcendentals=0,
         ),
         name="own_rows",
-    )(recv, w_up, w_down, stay(head))
-
+    )(recv, w_up, w_down, stay(head), stay(tokens))
+
+    peer_x, recv_g, part = lax.optimization_barrier((peer_x, recv[:, width:], part))
+    peer_g = to_peers(recv_g)
     others = rows * (copies - 1)
     x_peer, hidden_peer, slope_peer, scores = pl.pallas_call(
         functools.partial(peer_kernel, copies),
@@ -383,12 +461,12 @@
             shape((local_count, others, hidden_count), F32),
             shape((sources, lanes), F32),
         ),
-        in_specs=[VMEM] * 5,
+        in_specs=[VMEM] * 6,
         out_specs=(VMEM,) * 4,
         compiler_params=limit(16),
         cost_estimate=pl.CostEstimate(flops=2 * one_product, bytes_accessed=0, transcendentals=0),
         name="peer_rows",
-    )(peer_x, up_here, down_here, heads, part)
+    )(peer_x, up_here, down_first, down_rest, heads, part)
 
     returned = lax.all_to_all(
         scores.reshape(sources, 1, lanes),
@@ -398,9 +476,8 @@
         tiled=True,
     ).reshape(sources, lanes)
 
-    up_tile = math.gcd(width, 128)
-    down_tile = math.gcd(hidden_count, 256)
-    blocks = local_count * (width // up_tile + hidden_count // down_tile)
+    blocks = update_blocks(local_count, width, hidden_count)
+    up_tile, down_tile = [max(b[3] for b in blocks if b[1] == down) for down in (False, True)]
     updates = pl.pallas_call(
         functools.partial(update_kernel, copies),
         out_shape=(up_shape, down_shape, up_shape, up_shape, down_shape, down_shape),
@@ -414,7 +491,7 @@
             pltpu.VMEM((local_count, rows * copies, hidden_count), BF),
             pltpu.VMEM((2, up_tile, hidden_count), F32),
             pltpu.VMEM((2, down_tile, width), F32),
-            pltpu.SemaphoreType.DMA((2, blocks, 3)),
+            pltpu.SemaphoreType.DMA((2, len(blocks), 3)),
         ],
         compiler_params=limit(28),
         cost_estimate=pl.CostEstimate(
@@ -440,6 +517,7 @@
         down_square,
     )
 
+    returned, updates = lax.optimization_barrier((returned, updates))
     fine = pl.pallas_call(
         functools.partial(finish_kernel, holders),
         out_shape=shape((pixels, count), F32),

time: 43.2 us -> 42.5 us (0.984)
  waiting for transfers between devices: 0.63 us -> 0.01 us
    pallas_call x1, Pallas kernels: 11.4 us -> 10.7 us  [local(): pl.pallas_call(functools.partial(update_kernel, copies), out_shape=(up_sh...]
    ppermute x2, waiting for transfers between devices: 0.63 us -> 0.01 us  [to_peers(): lax.ppermute(value, 'dp', [(i, (i + step) % copies) for i in range(copies)])]
    ppermute x2, starting transfers between devices: 2.09 us -> 2.66 us  [to_peers(): lax.ppermute(value, 'dp', [(i, (i + step) % copies) for i in range(copies)])]
    pallas_call x1, Pallas kernels: 3.71 us -> 4.2 us  [local(): pl.pallas_call(own_kernel, out_shape=(shape((local_count, rows, width), B...]
  transfers between devices with their start and end apart: 3 -> 3, of which waited for: 1 -> 0; matrix products, arithmetic and copies ran while one was open for 0% -> 0% of each run, Pallas kernels for 40% -> 40%
where the time goes in v4:
time: 42.5 us; the launch traced here: 42.3 us
  Pallas kernels  19.1 us (45%)
  blocking collectives  17.2 us (40%)
  starting transfers between devices  5.2 us (12%)
  between operations  0.71 us (2%)
    all_to_all x1, blocking collectives, local(): lax.all_to_all(send, 'expert', split_axis=0, concat_axis=0, tiled=True)  17.2 us
    pallas_call x1, Pallas kernels, local(): pl.pallas_call(functools.partial(update_kernel, copies), out_shape=(up_sh...  10.7 us
    pallas_call x1, Pallas kernels, local(): pl.pallas_call(own_kernel, out_shape=(shape((local_count, rows, width), B...  4.2 us
    ppermute x2, starting transfers between devices, to_peers(): lax.ppermute(value, 'dp', [(i, (i + step) % copies) for i in range(copies)])  2.66 us
    all_to_all x1, starting transfers between devices, local(): lax.all_to_all(scores.reshape(sources, 1, lanes), ('dp', 'expert'), split...  2.54 us
    pallas_call x1, Pallas kernels, local(): pl.pallas_call(functools.partial(peer_kernel, copies), out_shape=(shape((...  1.95 us
    pallas_call x1, Pallas kernels, local(): pl.pallas_call(pack_kernel, out_shape=(shape((experts * CAP, 2 * width),...  1.34 us
    pallas_call x1, Pallas kernels, local(): pl.pallas_call(functools.partial(finish_kernel, holders), out_shape=shape...  0.9 us
  transfers between devices with their start and end apart: 3, of which 0 were waited for; matrix products, arithmetic and copies ran while one was open for 0% of the time, Pallas kernels for 40%

profile of v4, /device:TPU:0, one launch (start us, length us, event | category | flops | bytes accessed | tf_op | source)
XLA Modules:
  0.0 42.3 jit_solution(6539955023212316825)
XLA Ops:
  0.6 1.3 %pack.1 = (bf16[128,1024]{1,0:T(8,128)(2,1)S(1)}, s32[1,128]{1,0:T(1,128)S(1)}) custom-call(s32[1,128]{1,0:T(1,128)} %bitcast.17, s32[32]{0:T(128)} %placement.1, bf16[128,512]{1,0:T(8,128)(2,1)} %tokens.3, bf16[128,512]{1,0:T(8,128)(2,1)} %cotangent.1), custom_call_target="tpu_custom_call" | custom-call | tf_op jit(solution)/shard_map/pack/pallas_call | solution.py:397
  2.0 17.2 %all_to_all.16 = bf16[16,8,1024]{2,1,0:T(8,128)(2,1)S(1)} all-to-all(bf16[16,8,1024]{2,1,0:T(8,128)(2,1)S(1)} %bitcast.12), channel_id=1, replica_groups=mesh['dp'=2,'expert'=16] {'expert'}, dimensions={0} | all-to-all | bytes 524288 | tf_op jit(solution)/shard_map/all_to_all | solution.py:409
  19.2 1.6 %collective-permute-start = (bf16[128,512]{1,0:T(8,128)(2,1)S(1)}, bf16[128,512]{1,0:T(8,128)(2,1)S(1)}, u32[]{:S(2)}, u32[]{:S(2)}) collective-permute-start(bf16[128,512]{1,0:T(8,128)(2,1)S(1)} %get-tuple-element.72), channel_id=1, source_target_pairs={{0,16},{16,0},{1,17},{17,1},{2,18},{18,2},{3,19},{19,3},{4,20},{20... | collective-permute-start | bytes 393224 | tf_op jit(solution)/shard_map/ppermute | solution.py:413
  20.8 4.2 %own_rows.1 = (bf16[2,64,512]{2,1,0:T(8,128)(2,1)S(1)}, bf16[2,64,512]{2,1,0:T(8,128)(2,1)S(1)}, bf16[2,64,1024]{2,1,0:T(8,128)(2,1)S(1)}, f32[2,64,1024]{2,1,0:...) custom-call(bf16[128,1024]{1,0:T(8,128)(2,1)S(1)} %bitcast.11, ...), custom_call_target="tpu_custom_call" | custom-call | flops 536870912 | bytes 4194304 | tf_op jit(solution)/shard_map/own_rows/pallas_call | solution.py:422
  25.0 0.0 collective-permute-done.peers
  25.0 1.1 %collective-permute-start.1 = (bf16[128,512]{1,0:T(8,128)(2,1)S(1)}, bf16[128,512]{1,0:T(8,128)(2,1)S(1)}, u32[]{:S(2)}, u32[]{:S(2)}) collective-permute-start(bf16[128,512]{1,0:T(8,128)(2,1)S(1)} %get-tuple-element.52), channel_id=1, source_target_pairs={{0,16},{16,0},{1,17},{17,1},{2,18},{18,2},{3,19},{19,3},{4,20},{20... | collective-permute-start | bytes 393224 | tf_op jit(solution)/shard_map/ppermute | solution.py:413
  26.1 1.9 %peer_rows.1 = (bf16[2,64,512]{2,1,0:T(8,128)(2,1)S(1)}, bf16[2,64,1024]{2,1,0:T(8,128)(2,1)S(1)}, f32[2,64,1024]{2,1,0:T(8,128)S(1)}, f32[32,128]{1,0:T(8,128)}) custom-call(bf16[128,512]{1,0:T(8,128)(2,1)S(1)} %collective-permute-done.peers, bf16[2,512,1024]{2,1,0:T(8,128)(2,1)S(1)} %get-tuple-element.43.w_up, ...), custom_call_target="tpu_custom_call" | custom-call | flops 268435456 | tf_op jit(solution)/shard_map/peer_rows/pallas_call | solution.py:456
  28.1 2.5 %all-to-all-start.1 = ((f32[32,1,128]{2,1,0:T(1,128)}), f32[32,1,128]{2,1,0:T(1,128)S(1)}, u32[]{:S(2)}, u32[]{:S(2)}) async-start(f32[32,1,128]{2,1,0:T(1,128)} %bitcast.5), calls=%async_computation.1 | async-start | bytes 32768 | tf_op jit(solution)/shard_map/all_to_all | solution.py:471
  30.6 0.0 collective-permute-done.1.peer_g
  30.6 0.0 copy-start
  30.6 10.7 %update.1 = (bf16[2,512,1024]{2,1,0:T(8,128)(2,1)}, bf16[2,1024,512]{2,1,0:T(8,128)(2,1)}, bf16[2,512,1024]{2,1,0:T(8,128)(2,1)}, bf16[2,512,1024]{2,1,0:T(8,128...) custom-call(bf16[2,64,512]{2,1,0:T(8,128)(2,1)S(1)} %get-tuple-element.49.x_own, ...), custom_call_target="tpu_custom_call" | custom-call | flops 1610612736 | bytes 25165824 | tf_op jit(solution)/shard_map/update/pallas_call | solution.py:481
  41.4 0.0 all-to-all-done.1
  41.4 0.0 copy-done
  41.4 0.9 %finish.1 = f32[16,128]{1,0:T(8,128)} custom-call(s32[1,128]{1,0:T(1,128)S(1)} %get-tuple-element.39.slot, f32[32,128]{1,0:T(8,128)S(1)} %bitcast.13, f32[16,128]{1,0:T(8,128)S(1)} %get-tuple-element.64.own, f32[1,128]{1,0:T(1,128)S(1)} %bitcast.14), custom_call_target="tpu_custom_call" | custom-call | tf_op jit(solution)/shard_map/finish/pallas_call | solution.py:521
  (1 shorter events, 0.0 us)
Async XLA Ops:
  19.2 5.8 %collective-permute-start = (bf16[128,512]{1,0:T(8,128)(2,1)S(1)}, bf16[128,512]{1,0:T(8,128)(2,1)S(1)}, u32[]{:S(2)}, u32[]{:S(2)}) collective-permute-start(bf16[128,512]{1,0:T(8,128)(2,1)S(1)} %get-tuple-element.72), channel_id=1, source_target_pairs={{0,16},{16,0},{1,17},{17,1},{2,18},{18,2},{3,19},{19,3},{4,20},{20... | collective-permute-start | bytes 393224 | tf_op jit(solution)/shard_map/ppermute | solution.py:413
  25.0 5.6 %collective-permute-start.1 = (bf16[128,512]{1,0:T(8,128)(2,1)S(1)}, bf16[128,512]{1,0:T(8,128)(2,1)S(1)}, u32[]{:S(2)}, u32[]{:S(2)}) collective-permute-start(bf16[128,512]{1,0:T(8,128)(2,1)S(1)} %get-tuple-element.52), channel_id=1, source_target_pairs={{0,16},{16,0},{1,17},{17,1},{2,18},{18,2},{3,19},{19,3},{4,20},{20... | collective-permute-start | bytes 393224 | tf_op jit(solution)/shard_map/ppermute | solution.py:413
  28.1 13.3 %all-to-all-start.1 = ((f32[32,1,128]{2,1,0:T(1,128)}), f32[32,1,128]{2,1,0:T(1,128)S(1)}, u32[]{:S(2)}, u32[]{:S(2)}) async-start(f32[32,1,128]{2,1,0:T(1,128)} %bitcast.5), calls=%async_computation.1 | async-start | bytes 32768 | tf_op jit(solution)/shard_map/all_to_all | solution.py:471
  30.6 10.8 %copy-start = (f32[128]{0:T(128)S(1)}, f32[128]{0:T(128)}, u32[]{:S(2)}) copy-start(f32[128]{0:T(128)} %param.16) | copy-start | bytes 1540

commit v5 on v4

--- a/solution.py
+++ b/solution.py
@@ -137,12 +137,16 @@
         g_own[expert] = both[expert * rows : (expert + 1) * rows, width:]
     for copy in small:
         copy.wait()
-    rest = jnp.concatenate([head_here[...]] * (local_count * CAP), axis=0).T
+    rest = head_here[...]
+    pieces = []
     for i in range(3):
         piece = rest.astype(BF)
-        heads[i] = piece
+        pieces.append(piece)
+        heads[i] = jnp.concatenate([piece] * (local_count * CAP), axis=0).T
         rest = rest - piece.astype(F32)
-    own[...] = dot(head_here[...], tokens_here[...].astype(F32), ((1,), (1,)), EXACT)
+    pixels = head.shape[0]
+    terms = dot(jnp.concatenate(pieces, axis=0), tokens_here[...], ((1,), (1,)))
+    own[...] = terms[:pixels] + terms[pixels : 2 * pixels] + terms[2 * pixels :]
     for expert in range(local_count):
         copies[expert].wait()
         value, slant = gelu_parts(dot(x_own[expert], up_here[expert]))
@@ -450,8 +454,9 @@
         name="own_rows",
     )(recv, w_up, w_down, stay(head), stay(tokens))
 
-    peer_x, recv_g, part = lax.optimization_barrier((peer_x, recv[:, width:], part))
+    recv_g, part = lax.optimization_barrier((recv[:, width:], part))
     peer_g = to_peers(recv_g)
+    peer_x, part = lax.optimization_barrier((peer_x, part))
     others = rows * (copies - 1)
     x_peer, hidden_peer, slope_peer, scores = pl.pallas_call(
         functools.partial(peer_kernel, copies),

time: 42.5 us -> 41.8 us (0.984)
    ppermute x2, starting transfers between devices: 2.66 us -> 2.16 us  [to_peers(): lax.ppermute(value, 'dp', [(i, (i + step) % copies) for i in range(copies)])]
where the time goes in v5:
time: 41.8 us; the launch traced here: 41.6 us
  Pallas kernels  18.7 us (45%)
  blocking collectives  17.2 us (41%)
  starting transfers between devices  4.95 us (12%)
  between operations  0.7 us (2%)
    all_to_all x1, blocking collectives, local(): lax.all_to_all(send, 'expert', split_axis=0, concat_axis=0, tiled=True)  17.2 us
    pallas_call x1, Pallas kernels, local(): pl.pallas_call(functools.partial(update_kernel, copies), out_shape=(up_sh...  10.7 us
    pallas_call x1, Pallas kernels, local(): pl.pallas_call(own_kernel, out_shape=(shape((local_count, rows, width), B...  3.77 us
    all_to_all x1, starting transfers between devices, local(): lax.all_to_all(scores.reshape(sources, 1, lanes), ('dp', 'expert'), split...  2.79 us
    ppermute x2, starting transfers between devices, to_peers(): lax.ppermute(value, 'dp', [(i, (i + step) % copies) for i in range(copies)])  2.16 us
    pallas_call x1, Pallas kernels, local(): pl.pallas_call(functools.partial(peer_kernel, copies), out_shape=(shape((...  1.96 us
    pallas_call x1, Pallas kernels, local(): pl.pallas_call(pack_kernel, out_shape=(shape((experts * CAP, 2 * width),...  1.34 us
    pallas_call x1, Pallas kernels, local(): pl.pallas_call(functools.partial(finish_kernel, holders), out_shape=shape...  0.9 us
  transfers between devices with their start and end apart: 3, of which 0 were waited for; matrix products, arithmetic and copies ran while one was open for 0% of the time, Pallas kernels for 40%

profile of v5, /device:TPU:0, one launch (start us, length us, event | category | flops | bytes accessed | tf_op | source)
XLA Modules:
  0.0 41.6 jit_solution(7566371151910079201)
XLA Ops:
  0.6 1.3 %pack.1 = (bf16[128,1024]{1,0:T(8,128)(2,1)S(1)}, s32[1,128]{1,0:T(1,128)S(1)}) custom-call(s32[1,128]{1,0:T(1,128)} %bitcast.17, s32[32]{0:T(128)} %placement.1, bf16[128,512]{1,0:T(8,128)(2,1)} %tokens.3, bf16[128,512]{1,0:T(8,128)(2,1)} %cotangent.1), custom_call_target="tpu_custom_call" | custom-call | tf_op jit(solution)/shard_map/pack/pallas_call | solution.py:401
  2.0 17.2 %all_to_all.16 = bf16[16,8,1024]{2,1,0:T(8,128)(2,1)S(1)} all-to-all(bf16[16,8,1024]{2,1,0:T(8,128)(2,1)S(1)} %bitcast.12), channel_id=1, replica_groups=mesh['dp'=2,'expert'=16] {'expert'}, dimensions={0} | all-to-all | bytes 524288 | tf_op jit(solution)/shard_map/all_to_all | solution.py:413
  19.2 1.6 %collective-permute-start = (bf16[128,512]{1,0:T(8,128)(2,1)S(1)}, bf16[128,512]{1,0:T(8,128)(2,1)S(1)}, u32[]{:S(2)}, u32[]{:S(2)}) collective-permute-start(bf16[128,512]{1,0:T(8,128)(2,1)S(1)} %get-tuple-element.74), channel_id=1, source_target_pairs={{0,16},{16,0},{1,17},{17,1},{2,18},{18,2},{3,19},{19,3},{4,20},{20... | collective-permute-start | bytes 393224 | tf_op jit(solution)/shard_map/ppermute | solution.py:417
  20.8 3.8 %own_rows.1 = (bf16[2,64,512]{2,1,0:T(8,128)(2,1)S(1)}, bf16[2,64,512]{2,1,0:T(8,128)(2,1)S(1)}, bf16[2,64,1024]{2,1,0:T(8,128)(2,1)S(1)}, f32[2,64,1024]{2,1,0:...) custom-call(bf16[128,1024]{1,0:T(8,128)(2,1)S(1)} %bitcast.11, ...), custom_call_target="tpu_custom_call" | custom-call | flops 536870912 | bytes 4194304 | tf_op jit(solution)/shard_map/own_rows/pallas_call | solution.py:426
  24.6 0.6 %collective-permute-start.1 = (bf16[128,512]{1,0:T(8,128)(2,1)S(1)}, bf16[128,512]{1,0:T(8,128)(2,1)S(1)}, u32[]{:S(2)}, u32[]{:S(2)}) collective-permute-start(bf16[128,512]{1,0:T(8,128)(2,1)S(1)} %get-tuple-element.54), channel_id=1, source_target_pairs={{0,16},{16,0},{1,17},{17,1},{2,18},{18,2},{3,19},{19,3},{4,20},{20... | collective-permute-start | bytes 393224 | tf_op jit(solution)/shard_map/ppermute | solution.py:417
  25.2 0.0 collective-permute-done.peers
  25.2 2.0 %peer_rows.1 = (bf16[2,64,512]{2,1,0:T(8,128)(2,1)S(1)}, bf16[2,64,1024]{2,1,0:T(8,128)(2,1)S(1)}, f32[2,64,1024]{2,1,0:T(8,128)S(1)}, f32[32,128]{1,0:T(8,128)}) custom-call(bf16[128,512]{1,0:T(8,128)(2,1)S(1)} %collective-permute-done.peers, bf16[2,512,1024]{2,1,0:T(8,128)(2,1)S(1)} %get-tuple-element.45.w_up, ...), custom_call_target="tpu_custom_call" | custom-call | flops 268435456 | tf_op jit(solution)/shard_map/peer_rows/pallas_call | solution.py:461
  27.1 2.8 %all-to-all-start.1 = ((f32[32,1,128]{2,1,0:T(1,128)}), f32[32,1,128]{2,1,0:T(1,128)S(1)}, u32[]{:S(2)}, u32[]{:S(2)}) async-start(f32[32,1,128]{2,1,0:T(1,128)} %bitcast.5), calls=%async_computation.1 | async-start | bytes 32768 | tf_op jit(solution)/shard_map/all_to_all | solution.py:476
  29.9 0.0 collective-permute-done.1.peer_g
  29.9 0.0 copy-start
  30.0 10.7 %update.1 = (bf16[2,512,1024]{2,1,0:T(8,128)(2,1)}, bf16[2,1024,512]{2,1,0:T(8,128)(2,1)}, bf16[2,512,1024]{2,1,0:T(8,128)(2,1)}, bf16[2,512,1024]{2,1,0:T(8,128...) custom-call(bf16[2,64,512]{2,1,0:T(8,128)(2,1)S(1)} %get-tuple-element.51.x_own, ...), custom_call_target="tpu_custom_call" | custom-call | flops 1610612736 | bytes 25165824 | tf_op jit(solution)/shard_map/update/pallas_call | solution.py:486
  40.7 0.0 all-to-all-done.1
  40.7 0.0 copy-done
  40.7 0.9 %finish.1 = f32[16,128]{1,0:T(8,128)} custom-call(s32[1,128]{1,0:T(1,128)S(1)} %get-tuple-element.40.slot, f32[32,128]{1,0:T(8,128)S(1)} %bitcast.13, f32[16,128]{1,0:T(8,128)S(1)} %get-tuple-element.66.own, f32[1,128]{1,0:T(1,128)S(1)} %bitcast.14), custom_call_target="tpu_custom_call" | custom-call | tf_op jit(solution)/shard_map/finish/pallas_call | solution.py:526
  (1 shorter events, 0.0 us)
Async XLA Ops:
  19.2 5.9 %collective-permute-start = (bf16[128,512]{1,0:T(8,128)(2,1)S(1)}, bf16[128,512]{1,0:T(8,128)(2,1)S(1)}, u32[]{:S(2)}, u32[]{:S(2)}) collective-permute-start(bf16[128,512]{1,0:T(8,128)(2,1)S(1)} %get-tuple-element.74), channel_id=1, source_target_pairs={{0,16},{16,0},{1,17},{17,1},{2,18},{18,2},{3,19},{19,3},{4,20},{20... | collective-permute-start | bytes 393224 | tf_op jit(solution)/shard_map/ppermute | solution.py:417
  24.6 5.4 %collective-permute-start.1 = (bf16[128,512]{1,0:T(8,128)(2,1)S(1)}, bf16[128,512]{1,0:T(8,128)(2,1)S(1)}, u32[]{:S(2)}, u32[]{:S(2)}) collective-permute-start(bf16[128,512]{1,0:T(8,128)(2,1)S(1)} %get-tuple-element.54), channel_id=1, source_target_pairs={{0,16},{16,0},{1,17},{17,1},{2,18},{18,2},{3,19},{19,3},{4,20},{20... | collective-permute-start | bytes 393224 | tf_op jit(solution)/shard_map/ppermute | solution.py:417
  27.1 13.6 %all-to-all-start.1 = ((f32[32,1,128]{2,1,0:T(1,128)}), f32[32,1,128]{2,1,0:T(1,128)S(1)}, u32[]{:S(2)}, u32[]{:S(2)}) async-start(f32[32,1,128]{2,1,0:T(1,128)} %bitcast.5), calls=%async_computation.1 | async-start | bytes 32768 | tf_op jit(solution)/shard_map/all_to_all | solution.py:476
  29.9 10.8 %copy-start = (f32[128]{0:T(128)S(1)}, f32[128]{0:T(128)}, u32[]{:S(2)}) copy-start(f32[128]{0:T(128)} %param.16) | copy-start | bytes 1540

commit v6 on v5

--- a/solution.py
+++ b/solution.py
@@ -78,16 +78,21 @@
 
 
 def score_rows(expert, value, w_down, heads, local_count):
-    group = value.shape[0] // CAP
+    rows = value[0].shape[0]
+    group = rows // CAP
     lanes = heads.shape[2]
-    out = dot(value, w_down).astype(BF)
+    out = dot(jnp.concatenate(value, axis=0), w_down).astype(BF)
     logit = dot(out, heads[0]) + dot(out, heads[1]) + dot(out, heads[2])
     place = iota((group, lanes), 1) // (lanes // (local_count * CAP))
-    total = jnp.zeros((group, lanes), F32)
-    for c in range(CAP):
-        mine = place == expert * CAP + c
-        total = jnp.where(mine, logit[c * group : (c + 1) * group], total)
-    return total
+    totals = []
+    for start in range(0, rows * len(value), rows):
+        total = jnp.zeros((group, lanes), F32)
+        for c in range(CAP):
+            mine = place == expert * CAP + c
+            at = start + c * group
+            total = jnp.where(mine, logit[at : at + group], total)
+        totals.append(total)
+    return totals
 
 
 def own_kernel(
@@ -100,7 +105,6 @@
     g_own,
     hidden,
     slope,
-    part,
     heads,
     own,
     up_here,
@@ -152,17 +156,12 @@
         value, slant = gelu_parts(dot(x_own[expert], up_here[expert]))
         hidden[expert] = value.astype(BF)
         slope[expert] = slant
-    total = None
-    for expert in range(local_count):
-        copies[local_count + expert].wait()
-        weight = down_rest[expert - 1] if expert else down_first[...]
-        logit = score_rows(expert, hidden[expert], weight, heads, local_count)
-        total = logit if total is None else total + logit
-    part[...] = total
+    for copy in copies[local_count:]:
+        copy.wait()
 
 
 def peer_kernel(
-    copies, peers, w_up, down_first, down_rest, heads, part, x_peer, hidden, slope, out
+    copies, peers, w_up, down_first, down_rest, heads, hidden_own, x_peer, hidden, slope, out
 ):
     local_count = w_up.shape[0]
     span = peers.shape[0] // (copies - 1)
@@ -170,11 +169,10 @@
     group = rows // CAP
     here = lax.axis_index("dp")
     select = unmix(local_count, span)
-    out[pl.ds(pl.multiple_of(here * group, 8), group), :] = part[...]
     for step in range(1, copies):
         at = pl.ds((step - 1) * rows, rows)
         x = dot(select, peers[pl.ds((step - 1) * span, span), :]).astype(BF)
-        total = None
+        totals = None
         for expert in range(local_count):
             mine = x[expert * rows : (expert + 1) * rows]
             x_peer[expert, at, :] = mine
@@ -182,11 +180,13 @@
             value = value.astype(BF)
             hidden[expert, at, :] = value
             weight = down_rest[expert - 1] if expert else down_first[...]
-            logit = score_rows(expert, value, weight, heads, local_count)
             slope[expert, at, :] = slant
-            total = logit if total is None else total + logit
+            values = [value, hidden_own[expert]] if step == 1 else [value]
+            terms = score_rows(expert, values, weight, heads, local_count)
+            totals = terms if totals is None else [a + b for a, b in zip(totals, terms)]
         owner = lax.rem(here - step + copies, copies)
-        out[pl.ds(pl.multiple_of(owner * group, 8), group), :] = total
+        for place, total in zip((owner, here), totals):
+            out[pl.ds(pl.multiple_of(place * group, 8), group), :] = total
 
 
 def graded(total, small_first, small_last):
@@ -422,7 +422,7 @@
     peer_x = to_peers(recv[:, :width])
 
     (
-        x_own, g_own, hidden_own, slope_own, part, heads, own, up_here, down_first, down_rest
+        x_own, g_own, hidden_own, slope_own, heads, own, up_here, down_first, down_rest
     ) = pl.pallas_call(
         own_kernel,
         out_shape=(
@@ -430,7 +430,6 @@
             shape((local_count, rows, width), BF),
             shape((local_count, rows, hidden_count), BF),
             shape((local_count, rows, hidden_count), F32),
-            shape((holders, lanes), F32),
             pltpu.VMEM((3, width, lanes), BF),
             shape((pixels, count), F32),
             pltpu.VMEM(w_up.shape, BF),
@@ -438,7 +437,7 @@
             pltpu.VMEM((local_count - 1,) + w_down.shape[1:], BF),
         ),
         in_specs=[VMEM, HBM, HBM, HBM, HBM],
-        out_specs=(VMEM,) * 10,
+        out_specs=(VMEM,) * 9,
         scratch_shapes=[
             pltpu.VMEM(head.shape, F32),
             pltpu.VMEM(tokens.shape, BF),
@@ -454,9 +453,9 @@
         name="own_rows",
     )(recv, w_up, w_down, stay(head), stay(tokens))
 
-    recv_g, part = lax.optimization_barrier((recv[:, width:], part))
+    recv_g, heads = lax.optimization_barrier((recv[:, width:], heads))
     peer_g = to_peers(recv_g)
-    peer_x, part = lax.optimization_barrier((peer_x, part))
+    peer_x, heads = lax.optimization_barrier((peer_x, heads))
     others = rows * (copies - 1)
     x_peer, hidden_peer, slope_peer, scores = pl.pallas_call(
         functools.partial(peer_kernel, copies),
@@ -471,7 +470,7 @@
         compiler_params=limit(16),
         cost_estimate=pl.CostEstimate(flops=2 * one_product, bytes_accessed=0, transcendentals=0),
         name="peer_rows",
-    )(peer_x, up_here, down_first, down_rest, heads, part)
+    )(peer_x, up_here, down_first, down_rest, heads, hidden_own)
 
     returned = lax.all_to_all(
         scores.reshape(sources, 1, lanes),

time: 41.8 us -> 41.7 us (level)
  Pallas kernels: 18.7 us -> 17.8 us
    pallas_call x1, Pallas kernels: 3.77 us -> 2.81 us  [local(): pl.pallas_call(own_kernel, out_shape=(shape((local_count, rows, width), B...]
  transfers between devices with their start and end apart: 3 -> 3, of which waited for: 0 -> 1; matrix products, arithmetic and copies ran while one was open for 0% -> 0% of each run, Pallas kernels for 40% -> 37%
where the time goes in v6:
time: 41.7 us; the launch traced here: 41.5 us
  Pallas kernels  17.8 us (43%)
  blocking collectives  17.2 us (41%)
  starting transfers between devices  5.32 us (13%)
  between operations  0.7 us (2%)
    all_to_all x1, blocking collectives, local(): lax.all_to_all(send, 'expert', split_axis=0, concat_axis=0, tiled=True)  17.2 us
    pallas_call x1, Pallas kernels, local(): pl.pallas_call(functools.partial(update_kernel, copies), out_shape=(up_sh...  10.7 us
    all_to_all x1, starting transfers between devices, local(): lax.all_to_all(scores.reshape(sources, 1, lanes), ('dp', 'expert'), split...  3.16 us
    pallas_call x1, Pallas kernels, local(): pl.pallas_call(own_kernel, out_shape=(shape((local_count, rows, width), B...  2.81 us
    ppermute x2, starting transfers between devices, to_peers(): lax.ppermute(value, 'dp', [(i, (i + step) % copies) for i in range(copies)])  2.16 us
    pallas_call x1, Pallas kernels, local(): pl.pallas_call(functools.partial(peer_kernel, copies), out_shape=(shape((...  2.01 us
    pallas_call x1, Pallas kernels, local(): pl.pallas_call(pack_kernel, out_shape=(shape((experts * CAP, 2 * width),...  1.34 us
    pallas_call x1, Pallas kernels, local(): pl.pallas_call(functools.partial(finish_kernel, holders), out_shape=shape...  0.9 us
  transfers between devices with their start and end apart: 3, of which 1 were waited for; matrix products, arithmetic and copies ran while one was open for 0% of the time, Pallas kernels for 37%

profile of v6, /device:TPU:0, one launch (start us, length us, event | category | flops | bytes accessed | tf_op | source)
XLA Modules:
  0.0 41.5 jit_solution(14722166083607846558)
XLA Ops:
  0.6 1.3 %pack.1 = (bf16[128,1024]{1,0:T(8,128)(2,1)S(1)}, s32[1,128]{1,0:T(1,128)S(1)}) custom-call(s32[1,128]{1,0:T(1,128)} %bitcast.17, s32[32]{0:T(128)} %placement.1, bf16[128,512]{1,0:T(8,128)(2,1)} %tokens.3, bf16[128,512]{1,0:T(8,128)(2,1)} %cotangent.1), custom_call_target="tpu_custom_call" | custom-call | tf_op jit(solution)/shard_map/pack/pallas_call | solution.py:401
  2.0 17.2 %all_to_all.16 = bf16[16,8,1024]{2,1,0:T(8,128)(2,1)S(1)} all-to-all(bf16[16,8,1024]{2,1,0:T(8,128)(2,1)S(1)} %bitcast.12), channel_id=1, replica_groups=mesh['dp'=2,'expert'=16] {'expert'}, dimensions={0} | all-to-all | bytes 524288 | tf_op jit(solution)/shard_map/all_to_all | solution.py:413
  19.2 1.6 %collective-permute-start = (bf16[128,512]{1,0:T(8,128)(2,1)S(1)}, bf16[128,512]{1,0:T(8,128)(2,1)S(1)}, u32[]{:S(2)}, u32[]{:S(2)}) collective-permute-start(bf16[128,512]{1,0:T(8,128)(2,1)S(1)} %get-tuple-element.72), channel_id=1, source_target_pairs={{0,16},{16,0},{1,17},{17,1},{2,18},{18,2},{3,19},{19,3},{4,20},{20... | collective-permute-start | bytes 393224 | tf_op jit(solution)/shard_map/ppermute | solution.py:417
  20.8 2.8 %own_rows.1 = (bf16[2,64,512]{2,1,0:T(8,128)(2,1)S(1)}, bf16[2,64,512]{2,1,0:T(8,128)(2,1)S(1)}, bf16[2,64,1024]{2,1,0:T(8,128)(2,1)S(1)}, f32[2,64,1024]{2,1,0:...) custom-call(bf16[128,1024]{1,0:T(8,128)(2,1)S(1)} %bitcast.11, ...), custom_call_target="tpu_custom_call" | custom-call | flops 536870912 | bytes 4194304 | tf_op jit(solution)/shard_map/own_rows/pallas_call | solution.py:426
  23.6 0.6 %collective-permute-start.1 = (bf16[128,512]{1,0:T(8,128)(2,1)S(1)}, bf16[128,512]{1,0:T(8,128)(2,1)S(1)}, u32[]{:S(2)}, u32[]{:S(2)}) collective-permute-start(bf16[128,512]{1,0:T(8,128)(2,1)S(1)} %get-tuple-element.53), channel_id=1, source_target_pairs={{0,16},{16,0},{1,17},{17,1},{2,18},{18,2},{3,19},{19,3},{4,20},{20... | collective-permute-start | bytes 393224 | tf_op jit(solution)/shard_map/ppermute | solution.py:417
  24.2 0.4 collective-permute-done.peers
  24.6 2.0 %peer_rows.1 = (bf16[2,64,512]{2,1,0:T(8,128)(2,1)S(1)}, bf16[2,64,1024]{2,1,0:T(8,128)(2,1)S(1)}, f32[2,64,1024]{2,1,0:T(8,128)S(1)}, f32[32,128]{1,0:T(8,128)}) custom-call(bf16[128,512]{1,0:T(8,128)(2,1)S(1)} %collective-permute-done.peers, bf16[2,512,1024]{2,1,0:T(8,128)(2,1)S(1)} %get-tuple-element.44.w_up, ...), custom_call_target="tpu_custom_call" | custom-call | flops 268435456 | tf_op jit(solution)/shard_map/peer_rows/pallas_call | solution.py:460
  26.6 3.2 %all-to-all-start.1 = ((f32[32,1,128]{2,1,0:T(1,128)}), f32[32,1,128]{2,1,0:T(1,128)S(1)}, u32[]{:S(2)}, u32[]{:S(2)}) async-start(f32[32,1,128]{2,1,0:T(1,128)} %bitcast.5), calls=%async_computation.1 | async-start | bytes 32768 | tf_op jit(solution)/shard_map/all_to_all | solution.py:475
  29.8 0.0 collective-permute-done.1.peer_g
  29.8 0.0 copy-start
  29.8 10.7 %update.1 = (bf16[2,512,1024]{2,1,0:T(8,128)(2,1)}, bf16[2,1024,512]{2,1,0:T(8,128)(2,1)}, bf16[2,512,1024]{2,1,0:T(8,128)(2,1)}, bf16[2,512,1024]{2,1,0:T(8,128...) custom-call(bf16[2,64,512]{2,1,0:T(8,128)(2,1)S(1)} %get-tuple-element.50.x_own, ...), custom_call_target="tpu_custom_call" | custom-call | flops 1610612736 | bytes 25165824 | tf_op jit(solution)/shard_map/update/pallas_call | solution.py:485
  40.5 0.0 all-to-all-done.1
  40.6 0.0 copy-done
  40.6 0.9 %finish.1 = f32[16,128]{1,0:T(8,128)} custom-call(s32[1,128]{1,0:T(1,128)S(1)} %get-tuple-element.39.slot, f32[32,128]{1,0:T(8,128)S(1)} %bitcast.13, f32[16,128]{1,0:T(8,128)S(1)} %get-tuple-element.64.own, f32[1,128]{1,0:T(1,128)S(1)} %bitcast.14), custom_call_target="tpu_custom_call" | custom-call | tf_op jit(solution)/shard_map/finish/pallas_call | solution.py:525
  (1 shorter events, 0.0 us)
Async XLA Ops:
  19.2 5.4 %collective-permute-start = (bf16[128,512]{1,0:T(8,128)(2,1)S(1)}, bf16[128,512]{1,0:T(8,128)(2,1)S(1)}, u32[]{:S(2)}, u32[]{:S(2)}) collective-permute-start(bf16[128,512]{1,0:T(8,128)(2,1)S(1)} %get-tuple-element.72), channel_id=1, source_target_pairs={{0,16},{16,0},{1,17},{17,1},{2,18},{18,2},{3,19},{19,3},{4,20},{20... | collective-permute-start | bytes 393224 | tf_op jit(solution)/shard_map/ppermute | solution.py:417
  23.6 6.2 %collective-permute-start.1 = (bf16[128,512]{1,0:T(8,128)(2,1)S(1)}, bf16[128,512]{1,0:T(8,128)(2,1)S(1)}, u32[]{:S(2)}, u32[]{:S(2)}) collective-permute-start(bf16[128,512]{1,0:T(8,128)(2,1)S(1)} %get-tuple-element.53), channel_id=1, source_target_pairs={{0,16},{16,0},{1,17},{17,1},{2,18},{18,2},{3,19},{19,3},{4,20},{20... | collective-permute-start | bytes 393224 | tf_op jit(solution)/shard_map/ppermute | solution.py:417
  26.6 13.9 %all-to-all-start.1 = ((f32[32,1,128]{2,1,0:T(1,128)}), f32[32,1,128]{2,1,0:T(1,128)S(1)}, u32[]{:S(2)}, u32[]{:S(2)}) async-start(f32[32,1,128]{2,1,0:T(1,128)} %bitcast.5), calls=%async_computation.1 | async-start | bytes 32768 | tf_op jit(solution)/shard_map/all_to_all | solution.py:475
  29.8 10.8 %copy-start = (f32[128]{0:T(128)S(1)}, f32[128]{0:T(128)}, u32[]{:S(2)}) copy-start(f32[128]{0:T(128)} %param.16) | copy-start | bytes 1540
